TPU v7x, 32 devices: a whole 2x2x4 slice. The times are simulated.
32 devices in a mesh: row: 8 (over z, core), col: 4 (over y, x).
Axes of the slice: x: 2, y: 2, z: 4, core: 2. Of those that a mesh axis runs over, the one named last changes fastest.
Arguments:
- reflectivity: float32 [32, 256, 1024], P(('row', 'col')), may hold values from 0 to 40
- scan_hour: int32 [32], replicated, may hold values from 0 to 3, as said below
- basin_ids: int32 [256, 8], P('row', 'col'), may hold values from 0 to 255, as said below
Outputs:
- hourly_depth: float32 [4, 256, 1024], P(None, 'row', 'col')
- basin_depth: float32 [256, 4], P(('row', 'col'))
Inputs may be any that keep to these rules, and one draw needn't show every extreme that they name: scan_hour starts at 0, never falls, rises by at most one from one scan to the next, and every hour has 1 to 12 scans. `basin_ids`: every basin is named by at least one segment, and all segments of a basin lie in one aligned block of 8 grid rows.
All inputs are finite; a program needn't handle non-finite values.
Results may differ from a plain program's by a relative error of at most 0.00021.
Values sent between devices are 32-bit elements; how exact they have to be, the bound alone decides.
A program may use at most 64 MiB of HBM per device.

v0:
```python
import functools
import math

import jax
import jax.numpy as jnp
from jax import lax
from jax.experimental import pallas as pl
from jax.experimental.pallas import tpu as pltpu
from jax.sharding import PartitionSpec as P

SEG = 128
BASIN_ROWS = 8
HOUR_SCANS = 12
CORES = 2
MESH = pl.DeviceIdType.MESH

slope_db = math.log(10.0) / 16.0
offset_zr = math.log(200.0) / 1.6 + math.log(12.0)


def kernel(
    dims,
    refl_ref,
    hour_ref,
    ids_ref,
    hourly_ref,
    basin_ref,
    frame,
    hours,
    ids,
    gather,
    part,
    zrecv,
    plane_ids,
    all_ids,
    psend,
    precv,
    relay_sem,
    local_sem,
    own_sem,
    in_send,
    in_recv,
    z_send,
    z_recv,
    id_send,
    id_recv,
    idz_send,
    idz_recv,
    b_send,
    b_recv,
):
    row_devices, col_devices, hour_count, slots, tile_rows, tile_cols, owned = dims
    planes = row_devices // CORES
    members = CORES * col_devices
    devices = row_devices * col_devices
    scan_block = gather.shape[2]
    scan_count = hour_ref.shape[0]
    plane_scans = members * scan_block
    segs = tile_cols // SEG

    row = lax.axis_index("row")
    col = lax.axis_index("col")
    plane = row // CORES
    core = row % CORES
    mine = core * col_devices + col
    me = row * col_devices + col

    def first_hour(p):
        return (p * plane_scans) // HOUR_SCANS

    def hour_span(p):
        tail = scan_count - plane_scans - p * plane_scans
        return hour_count - tail // HOUR_SCANS - first_hour(p)

    def member_at(k):
        dc = k // col_devices
        dq = k % col_devices
        half = col_devices // 2
        qq = ((col // 2 + dq // 2) % half) * 2 + (col + dq) % 2
        other = ((core + dc) % CORES) * col_devices + qq
        return other, plane * CORES + other // col_devices, other % col_devices

    load_frame = pltpu.make_async_copy(refl_ref, frame, local_sem.at[0])
    load_hours = pltpu.make_async_copy(hour_ref, hours, local_sem.at[1])
    load_ids = pltpu.make_async_copy(ids_ref, ids, local_sem.at[2])
    load_frame.start()
    load_hours.start()
    load_ids.start()
    load_own_ids = pltpu.make_async_copy(
        ids_ref, plane_ids.at[core * col_devices + col], local_sem.at[3]
    )
    load_own_ids.start()

    def block_of(source, d, c, q):
        rows = pl.ds(pl.multiple_of((d * CORES + c) * tile_rows, 8), tile_rows)
        cols = pl.ds(pl.multiple_of(q * tile_cols, 128), tile_cols)
        return source.at[:, rows, cols]

    barrier = pltpu.get_barrier_semaphore()
    for k in range(1, members):
        _, r, q = member_at(k)
        pl.semaphore_signal(barrier, inc=1, device_id=(r, q), device_id_type=MESH)
    def along_z(step):
        return ((plane + step) * CORES + core, col)

    @pl.when(plane > 0)
    def _():
        pl.semaphore_signal(barrier, inc=1, device_id=along_z(-1), device_id_type=MESH)

    @pl.when(plane < planes - 1)
    def _():
        pl.semaphore_signal(barrier, inc=1, device_id=along_z(1), device_id_type=MESH)

    own_copies = []
    for d in range(planes):
        own = pltpu.make_async_copy(
            block_of(refl_ref, d, core, col), gather.at[d, mine], own_sem.at[d]
        )
        own.start()
        own_copies.append(own)

    low = plane < planes // 2
    order = []
    for t in range(planes - 1):
        down = planes - 1 - t
        down = jnp.where(down > plane, down, down - 1)
        up = jnp.where(t < plane, t, t + 1)
        order.append(jnp.where(low, down, up))
    order.append(plane)

    load_ids.wait()
    load_frame.wait()
    beside = jnp.where(plane > 0, 1, 0) + jnp.where(plane < planes - 1, 1, 0)
    pl.semaphore_wait(barrier, members - 1 + beside)

    def id_copy(k):
        other, r, q = member_at(k)
        return pltpu.make_async_remote_copy(
            src_ref=ids,
            dst_ref=plane_ids.at[mine],
            send_sem=id_send.at[other],
            recv_sem=id_recv.at[mine],
            device_id=(r, q),
            device_id_type=MESH,
        )

    for k in range(1, members):
        id_copy(k).start()

    def in_copy(d, k):
        other, r, q = member_at(k)
        return pltpu.make_async_remote_copy(
            src_ref=block_of(frame, d, other // col_devices, q),
            dst_ref=gather.at[d, mine],
            send_sem=in_send.at[d, other],
            recv_sem=in_recv.at[d, mine],
            device_id=(r, q),
            device_id_type=MESH,
        )

    def in_arrival(d, k):
        other, r, q = member_at(k)
        return pltpu.make_async_remote_copy(
            src_ref=gather.at[d, other],
            dst_ref=gather.at[d, other],
            send_sem=in_send.at[d, other],
            recv_sem=in_recv.at[d, other],
            device_id=(r, q),
            device_id_type=MESH,
        )

    def send_chunk(d):
        for k in range(1, members):
            in_copy(d, k).start()

    early = max(1, planes - 1)
    for d in order[:early]:
        send_chunk(d)

    for j in range(planes - 2):

        @pl.when(plane > 0)
        def _():
            pl.semaphore_signal(
                relay_sem.at[1, j], inc=1, device_id=along_z(-1), device_id_type=MESH
            )

        @pl.when(plane < planes - 1)
        def _():
            pl.semaphore_signal(
                relay_sem.at[0, j], inc=1, device_id=along_z(1), device_id_type=MESH
            )

        @pl.when(plane > 0)
        def _():
            pl.semaphore_wait(relay_sem.at[0, j], 1)

        @pl.when(plane < planes - 1)
        def _():
            pl.semaphore_wait(relay_sem.at[1, j], 1)

    for k in range(1, members):
        other, r, q = member_at(k)
        pltpu.make_async_remote_copy(
            src_ref=ids,
            dst_ref=plane_ids.at[other],
            send_sem=id_send.at[other],
            recv_sem=id_recv.at[other],
            device_id=(r, q),
            device_id_type=MESH,
        ).wait_recv()
    load_own_ids.wait()

    def idz_copy(k, arrival=False):
        other = (plane + k) % planes
        return pltpu.make_async_remote_copy(
            src_ref=plane_ids,
            dst_ref=all_ids.at[other if arrival else plane],
            send_sem=idz_send.at[other],
            recv_sem=idz_recv.at[other if arrival else plane],
            device_id=(other * CORES + core, col),
            device_id_type=MESH,
        )

    for k in range(1, planes):
        idz_copy(k).start()
    all_ids[plane] = plane_ids[...]
    load_hours.wait()
    for own in own_copies:
        own.wait()

    base_hour = first_hour(plane)
    span = hour_span(plane)

    def z_copy(d, k):
        return pltpu.make_async_remote_copy(
            src_ref=part.at[d, k],
            dst_ref=zrecv.at[plane, k],
            send_sem=z_send.at[d, k],
            recv_sem=z_recv.at[plane, k],
            device_id=(d * CORES + core, col),
            device_id_type=MESH,
        )

    def b_copy(k):
        other = (me + k) % devices
        return pltpu.make_async_remote_copy(
            src_ref=psend,
            dst_ref=precv.at[me],
            send_sem=b_send.at[other],
            recv_sem=b_recv.at[me],
            device_id=(other // col_devices, other % col_devices),
            device_id_type=MESH,
        )

    basins = psend.shape[1]

    def sum_basins():
        lane = lax.broadcasted_iota(jnp.int32, (tile_rows, basins), 1)

        def row_block(r, carry):
            count, *totals = carry
            p = r // CORES
            c = r % CORES
            depths = []
            for b in range(scan_block):
                rows = pl.ds(pl.multiple_of(r * tile_rows, 8), tile_rows)
                depths.append(jnp.exp(frame[b, rows, :] * slope_db - offset_zr))
            tiles = [all_ids[p, c * col_devices + q] for q in range(col_devices)]
            columns = jnp.transpose(jnp.concatenate(tiles, axis=0).astype(jnp.float32))
            columns = columns.astype(jnp.int32)
            for g in range(segs * col_devices):
                hit = columns[:, g : g + 1] == lane
                count = count + jnp.where(hit, float(SEG), 0.0)
                for b in range(scan_block):
                    part_depth = depths[b][:, g * SEG : (g + 1) * SEG]
                    value = jnp.sum(part_depth, axis=1, keepdims=True)
                    totals[b] = totals[b] + jnp.where(hit, value, 0.0)
            return (count, *totals)

        zero = jnp.zeros((tile_rows, basins), jnp.float32)
        count, *totals = lax.fori_loop(
            0, row_devices, row_block, (zero,) * (scan_block + 1), unroll=4
        )
        for b in range(scan_block):
            psend[b : b + 1, :] = jnp.sum(totals[b], axis=0, keepdims=True)
        return jnp.sum(count, axis=0, keepdims=True)

    count = None
    for t, d in enumerate(order):
        if t == min(1, planes - 1):
            for k in range(1, planes):
                idz_copy(k, arrival=True).wait_recv()
            count = sum_basins()

            def b_start(k, carry):
                b_copy(k).start()
                return carry

            lax.fori_loop(1, devices, b_start, 0, unroll=True)
            precv[me] = psend[...]
            for late in order[early:]:
                send_chunk(late)
        for k in range(1, members):
            in_arrival(d, k).wait_recv()
        sums = [jnp.zeros((tile_rows, tile_cols), jnp.float32)] * slots
        for i in range(members):
            for b in range(scan_block):
                hour = hours[plane * plane_scans + i * scan_block + b] - base_hour
                depth = jnp.exp(gather[d, i, b] * slope_db - offset_zr)
                for k in range(slots):
                    sums[k] = sums[k] + jnp.where(hour == k, depth, 0.0)
        if t < planes - 1:
            for k in range(slots):
                part[d, k] = sums[k]
            for k in range(slots):

                @pl.when(k < span)
                def _():
                    z_copy(d, k).start()

        else:
            for k in range(slots):
                zrecv[plane, k] = sums[k]

    for p in range(planes):

        @pl.when(p != plane)
        def _():
            for k in range(hour_span(p)):
                pltpu.make_async_remote_copy(
                    src_ref=zrecv.at[p, k],
                    dst_ref=zrecv.at[p, k],
                    send_sem=z_send.at[p, k],
                    recv_sem=z_recv.at[p, k],
                    device_id=(p * CORES + core, col),
                    device_id_type=MESH,
                ).wait_recv()

    for h in range(hour_count):
        total = None
        for p in range(planes):
            if first_hour(p) <= h < first_hour(p) + hour_span(p):
                term = zrecv[p, h - first_hour(p)]
                total = term if total is None else total + term
        hourly_ref[h] = total

    for k in range(1, members):
        id_copy(k).wait_send()
    for k in range(1, planes):
        idz_copy(k).wait_send()
    for d in order:
        for k in range(1, members):
            in_copy(d, k).wait_send()
    for d in order[:-1]:
        for k in range(slots):

            @pl.when(k < span)
            def _():
                z_copy(d, k).wait_send()

    def b_wait(k, carry):
        other = (me + k) % devices
        arrival = pltpu.make_async_remote_copy(
            src_ref=psend,
            dst_ref=precv.at[other],
            send_sem=b_send.at[other],
            recv_sem=b_recv.at[other],
            device_id=(other // col_devices, other % col_devices),
            device_id_type=MESH,
        )
        arrival.wait_recv()
        arrival.wait_send()
        return carry

    lax.fori_loop(1, devices, b_wait, 0, unroll=True)
    hour_rows = lax.broadcasted_iota(jnp.int32, (hour_count, basins), 0)
    total = jnp.zeros((hour_count, basins), jnp.float32)
    for o in range(devices):
        for b in range(scan_block):
            hour = hours[o * scan_block + b]
            total = total + jnp.where(hour_rows == hour, precv[o, b : b + 1, :], 0.0)
    mean = total / count
    mean = pltpu.roll(mean, (basins - me * owned) % basins, 1)
    basin_ref[...] = mean[:, :owned]


def write_out(hourly_ref, basin_ref, hourly_out, basin_out, sem):
    pairs = ((hourly_ref, hourly_out), (basin_ref, basin_out))
    copies = [pltpu.make_async_copy(s, d, sem.at[n]) for n, (s, d) in enumerate(pairs)]
    for copy in copies:
        copy.start()
    for copy in copies:
        copy.wait()


def body(reflectivity, scan_hour, basin_ids):
    row_devices = lax.axis_size("row")
    col_devices = lax.axis_size("col")
    scan_block, grid_height, grid_width = reflectivity.shape
    tile_rows = grid_height // row_devices
    tile_cols = grid_width // col_devices
    scan_count = scan_hour.shape[0]
    hour_count = (scan_count + 10) // HOUR_SCANS + 1
    devices = row_devices * col_devices
    owned = grid_height * grid_width // (SEG * BASIN_ROWS) // devices
    planes = row_devices // CORES
    members = CORES * col_devices
    plane_scans = members * scan_block
    slots = max(
        hour_count
        - (scan_count - plane_scans * (p + 1)) // HOUR_SCANS
        - (p * plane_scans) // HOUR_SCANS
        for p in range(planes)
    )
    dims = (row_devices, col_devices, hour_count, slots, tile_rows, tile_cols, owned)
    dma = pltpu.SemaphoreType.DMA
    f32 = jnp.float32
    anywhere = pl.BlockSpec(memory_space=pltpu.HBM)
    inside = pl.BlockSpec(memory_space=pltpu.VMEM)
    hourly, basin = pl.pallas_call(
        functools.partial(kernel, dims),
        out_shape=(
            jax.ShapeDtypeStruct((hour_count, tile_rows, tile_cols), f32),
            jax.ShapeDtypeStruct((hour_count, owned), f32),
        ),
        in_specs=[anywhere] * 3,
        out_specs=(inside, inside),
        scratch_shapes=[
            pltpu.VMEM(reflectivity.shape, f32),
            pltpu.SMEM(scan_hour.shape, jnp.int32),
            pltpu.VMEM(basin_ids.shape[::-1], jnp.int32),
            pltpu.VMEM((planes, members, scan_block, tile_rows, tile_cols), f32),
            pltpu.VMEM((planes, slots, tile_rows, tile_cols), f32),
            pltpu.VMEM((planes, slots, tile_rows, tile_cols), f32),
            pltpu.VMEM((members,) + basin_ids.shape[::-1], jnp.int32),
            pltpu.VMEM((planes, members) + basin_ids.shape[::-1], jnp.int32),
            pltpu.VMEM((scan_block, devices * owned), f32),
            pltpu.VMEM((devices, scan_block, devices * owned), f32),
            pltpu.SemaphoreType.REGULAR((2, max(1, planes - 2))),
            dma((4,)),
            dma((planes,)),
            dma((planes, members)),
            dma((planes, members)),
            dma((planes, slots)),
            dma((planes, slots)),
            dma((members,)),
            dma((members,)),
            dma((planes,)),
            dma((planes,)),
            dma((devices,)),
            dma((devices,)),
        ],
        compiler_params=pltpu.CompilerParams(
            collective_id=0, has_side_effects=True, vmem_limit_bytes=40 * 2**20
        ),
    )(*(pltpu.with_memory_space_constraint(v, pltpu.HBM) for v in (reflectivity, scan_hour, basin_ids.T)))
    hourly, basin = pl.pallas_call(
        write_out,
        out_shape=(
            jax.ShapeDtypeStruct(hourly.shape, f32),
            jax.ShapeDtypeStruct(basin.shape, f32),
        ),
        in_specs=[inside] * 2,
        out_specs=(anywhere, anywhere),
        scratch_shapes=[dma((2,))],
        compiler_params=pltpu.CompilerParams(vmem_limit_bytes=8 * 2**20),
    )(hourly, basin)
    return hourly, basin.T


def solution(mesh):
    placed = (P(("row", "col"), None, None), P(), P("row", "col"))
    return jax.shard_map(
        body,
        mesh=mesh,
        in_specs=placed,
        out_specs=(P(None, "row", "col"), P(("row", "col"), None)),
        check_vma=False,
    )
```

profile of v0, /device:TPU:0, one launch (start us, length us, event | category | flops | bytes accessed | tf_op | source)
XLA Modules:
  0.0 22.8 jit_solution(7670245870127882282)
XLA Ops:
  0.6 21.5 %shard_map.50 = (f32[4,32,256]{2,1,0:T(8,128)S(1)}, f32[4,8]{1,0:T(4,128)S(1)}) custom-call(f32[1,256,1024]{2,1,0:T(8,128)} %refl_ref.1, s32[32]{0:T(128)} %hour_ref.1, s32[2,32]{1,0:T(2,128)} %bitcast.2), custom_call_target="tpu_custom_call" | custom-call | tf_op jit(solution)/shard_map/pallas_call | solution.py:421
  22.1 0.7 %shard_map.51 = (f32[4,32,256]{2,1,0:T(8,128)}, f32[4,8]{1,0:T(4,128)}) custom-call(f32[4,32,256]{2,1,0:T(8,128)S(1)} %get-tuple-element.6.hourly_ref, f32[4,8]{1,0:T(4,128)S(1)} %get-tuple-element.7.basin_ref), custom_call_target="tpu_custom_call" | custom-call | tf_op jit(solution)/shard_map/pallas_call | solution.py:458
where the time goes:
time: 23 us; the launch traced here: 22.8 us
  Pallas kernels  22.2 us (97%)
  between operations  0.64 us (3%)
    pallas_call x1, Pallas kernels, body(): pl.pallas_call(functools.partial(kernel, dims), out_shape=(jax.ShapeDtype...  21.5 us
    pallas_call x1, Pallas kernels, body(): pl.pallas_call(write_out, out_shape=(jax.ShapeDtypeStruct(hourly.shape, f...  0.68 us

commit v1 on v0

v1 whole, which is shorter than its diff:
```python
import functools
import math

import jax
import jax.numpy as jnp
from jax import lax
from jax.experimental import pallas as pl
from jax.experimental.pallas import tpu as pltpu
from jax.sharding import PartitionSpec as P

SEG = 128
BASIN_ROWS = 8
HOUR_SCANS = 12
CORES = 2
LANES = 128
HELD = 1
MESH = pl.DeviceIdType.MESH

slope_db = math.log(10.0) / 16.0
offset_zr = math.log(200.0) / 1.6 + math.log(12.0)


def kernel(
    dims,
    refl_ref,
    hour_ref,
    ids_ref,
    hourly_ref,
    basin_ref,
    frame,
    hours,
    ids,
    gather,
    part,
    zrecv,
    plane_ids,
    all_ids,
    psend,
    pcount,
    precv,
    wave_sem,
    local_sem,
    load_sem,
    own_sem,
    in_send,
    in_recv,
    z_send,
    z_recv,
    id_send,
    id_recv,
    idz_send,
    idz_recv,
    b_send,
    b_recv,
):
    row_devices, col_devices, hour_count, slots, tile_rows, tile_cols, owned = dims
    planes = row_devices // CORES
    members = CORES * col_devices
    devices = row_devices * col_devices
    scan_block = gather.shape[2]
    scan_count = hour_ref.shape[0]
    plane_scans = members * scan_block
    segs = tile_cols // SEG
    basins = devices * owned
    width = precv.shape[2]

    row = lax.axis_index("row")
    col = lax.axis_index("col")
    plane = row // CORES
    core = row % CORES
    mine = core * col_devices + col
    me = row * col_devices + col

    def first_hour(p):
        return (p * plane_scans) // HOUR_SCANS

    def hour_span(p):
        rest = scan_count - plane_scans - p * plane_scans
        return hour_count - rest // HOUR_SCANS - first_hour(p)

    def by_plane(table):
        value = table[0]
        for p in range(1, planes):
            value = jnp.where(plane == p, table[p], value)
        return value

    def chunk_order(p):
        others = sorted((d for d in range(planes) if d != p), key=lambda d: -abs(d - p))
        if 0 in others:
            others.remove(0)
            others.insert(0, 0)
        return others + [p]

    def near_order(p):
        return sorted(range(planes), key=lambda d: abs(d - p))

    orders = [chunk_order(p) for p in range(planes)]
    order = [by_plane([o[t] for o in orders]) for t in range(planes)]
    nears = [near_order(p) for p in range(planes)]
    near = [by_plane([o[t] for o in nears]) for t in range(planes)]

    def member_at(k):
        dc = k // col_devices
        dq = k % col_devices
        half = col_devices // 2
        qq = ((col // 2 + dq // 2) % half) * 2 + (col + dq) % 2
        other = ((core + dc) % CORES) * col_devices + qq
        return other, plane * CORES + other // col_devices, other % col_devices

    def several(ref, send_sem, recv_sem):
        return pltpu.make_async_remote_copy(
            src_ref=ref,
            dst_ref=ref,
            send_sem=send_sem,
            recv_sem=recv_sem,
            device_id=((row + 1) % row_devices, col),
            device_id_type=MESH,
        )

    def along_z(step):
        return ((plane + step) * CORES + core, col)

    barrier = pltpu.get_barrier_semaphore()
    for k in range(1, members):
        _, r, q = member_at(k)
        pl.semaphore_signal(barrier, inc=1, device_id=(r, q), device_id_type=MESH)

    @pl.when(plane > 0)
    def _():
        pl.semaphore_signal(barrier, inc=1, device_id=along_z(-1), device_id_type=MESH)

    @pl.when(plane < planes - 1)
    def _():
        pl.semaphore_signal(barrier, inc=1, device_id=along_z(1), device_id_type=MESH)

    def block_of(source, d, c, q):
        rows = pl.ds(pl.multiple_of((d * CORES + c) * tile_rows, 8), tile_rows)
        cols = pl.ds(pl.multiple_of(q * tile_cols, 128), tile_cols)
        return source.at[:, rows, cols]

    def plane_rows(d):
        rows = CORES * tile_rows
        return pl.ds(pl.multiple_of(d * rows, 8), rows)

    load_ids = pltpu.make_async_copy(ids_ref, ids, local_sem.at[0])
    load_ids.start()
    loads = []
    for t, d in enumerate(order):
        load = pltpu.make_async_copy(
            refl_ref.at[:, plane_rows(d), :],
            frame.at[:, plane_rows(d), :],
            load_sem.at[t],
        )
        load.start()
        loads.append(load)
    load_own_ids = pltpu.make_async_copy(
        ids_ref, plane_ids.at[mine], local_sem.at[1]
    )
    load_own_ids.start()
    load_hours = pltpu.make_async_copy(hour_ref, hours, local_sem.at[2])
    load_hours.start()
    for d in range(planes):
        own = pltpu.make_async_copy(
            block_of(refl_ref, d, core, col), gather.at[d, mine], own_sem
        )
        own.start()

    for k in range(slots):
        zrecv[plane, k] = jnp.zeros((tile_rows, tile_cols), jnp.float32)

    load_ids.wait()
    beside = jnp.where(plane > 0, 1, 0) + jnp.where(plane < planes - 1, 1, 0)
    pl.semaphore_wait(barrier, members - 1 + beside)

    def id_copy(k):
        other, r, q = member_at(k)
        return pltpu.make_async_remote_copy(
            src_ref=ids,
            dst_ref=plane_ids.at[mine],
            send_sem=id_send,
            recv_sem=id_recv,
            device_id=(r, q),
            device_id_type=MESH,
        )

    for k in range(1, members):
        id_copy(k).start()

    @pl.when((plane == 1) & (plane < planes - 1))
    def _():
        pl.semaphore_signal(
            wave_sem.at[0], inc=1, device_id=along_z(1), device_id_type=MESH
        )

    @pl.when((plane == planes - 2) & (plane > 0))
    def _():
        pl.semaphore_signal(
            wave_sem.at[1], inc=1, device_id=along_z(-1), device_id_type=MESH
        )

    def in_copy(d, k):
        other, r, q = member_at(k)
        return pltpu.make_async_remote_copy(
            src_ref=block_of(frame, d, other // col_devices, q),
            dst_ref=gather.at[d, mine],
            send_sem=in_send,
            recv_sem=in_recv.at[d],
            device_id=(r, q),
            device_id_type=MESH,
        )

    def in_arrival(d):
        return several(gather.at[d, pl.ds(0, members - 1)], in_send, in_recv.at[d])

    def send_chunk(t):
        for k in range(1, members):
            in_copy(order[t], k).start()

    early = max(1, planes - HELD)
    for t in range(early):
        loads[t].wait()
        send_chunk(t)
    for t in range(early, planes):
        loads[t].wait()


    @pl.when(plane >= 2)
    def _():
        pl.semaphore_wait(wave_sem.at[0], 1)

        @pl.when(plane < planes - 1)
        def _():
            pl.semaphore_signal(
                wave_sem.at[0], inc=1, device_id=along_z(1), device_id_type=MESH
            )

    @pl.when(plane < planes - 2)
    def _():
        pl.semaphore_wait(wave_sem.at[1], 1)

        @pl.when(plane > 0)
        def _():
            pl.semaphore_signal(
                wave_sem.at[1], inc=1, device_id=along_z(-1), device_id_type=MESH
            )

    several(plane_ids.at[pl.ds(0, members - 1)], id_send, id_recv).wait_recv()
    load_own_ids.wait()

    def idz_copy(k):
        other = (plane + k) % planes
        return pltpu.make_async_remote_copy(
            src_ref=plane_ids,
            dst_ref=all_ids.at[plane],
            send_sem=idz_send,
            recv_sem=idz_recv.at[plane],
            device_id=(other * CORES + core, col),
            device_id_type=MESH,
        )

    def idz_arrival(p):
        return several(all_ids.at[p], idz_send, idz_recv.at[p])

    for k in range(1, planes):
        idz_copy(k).start()
    all_ids[plane] = plane_ids[...]
    load_hours.wait()
    pltpu.make_async_copy(gather.at[:, 0], gather.at[:, 0], own_sem).wait()

    base_hour = first_hour(plane)
    span = hour_span(plane)

    def z_copy(d, k):
        return pltpu.make_async_remote_copy(
            src_ref=part.at[d, k],
            dst_ref=zrecv.at[plane, k],
            send_sem=z_send,
            recv_sem=z_recv.at[plane],
            device_id=(d * CORES + core, col),
            device_id_type=MESH,
        )

    def owner_lanes(o):
        return pl.ds(pl.multiple_of(((o * owned) // width) * width, width), width)

    def b_copy(k):
        other = (me + k) % devices
        return pltpu.make_async_remote_copy(
            src_ref=psend.at[:, owner_lanes(other)],
            dst_ref=precv.at[me],
            send_sem=b_send,
            recv_sem=b_recv,
            device_id=(other // col_devices, other % col_devices),
            device_id_type=MESH,
        )

    def depth_of(raw):
        return jnp.exp(raw * slope_db - offset_zr)

    def sum_rows(p, carry):
        lane = lax.broadcasted_iota(jnp.int32, (tile_rows, basins), 1)
        count, *totals = carry
        for c in range(CORES):
            depths = []
            for b in range(scan_block):
                rows = pl.ds(
                    pl.multiple_of((p * CORES + c) * tile_rows, 8), tile_rows
                )
                depths.append(depth_of(frame[b, rows, :]))
            tiles = [all_ids[p, c * col_devices + q] for q in range(col_devices)]
            columns = jnp.transpose(jnp.concatenate(tiles, axis=0).astype(jnp.float32))
            columns = columns.astype(jnp.int32)
            for g in range(segs * col_devices):
                hit = columns[:, g : g + 1] == lane
                count = count + jnp.where(hit, float(SEG), 0.0)
                for b in range(scan_block):
                    part_depth = depths[b][:, g * SEG : (g + 1) * SEG]
                    value = jnp.sum(part_depth, axis=1, keepdims=True)
                    totals[b] = totals[b] + jnp.where(hit, value, 0.0)
        return (count, *totals)

    def chunk_sums(d):
        sums = [jnp.zeros((tile_rows, tile_cols), jnp.float32)] * slots
        for i in range(members):
            for b in range(scan_block):
                hour = hours[plane * plane_scans + i * scan_block + b] - base_hour
                depth = depth_of(gather[d, i, b])
                for k in range(slots):
                    sums[k] = sums[k] + jnp.where(hour == k, depth, 0.0)
        return sums

    def push_chunk(t):
        d = order[t]
        in_arrival(d).wait_recv()
        sums = chunk_sums(d)
        for k in range(slots):
            part[d, k] = sums[k]
        for k in range(slots):

            @pl.when(k < span)
            def _():
                z_copy(d, k).start()

    def spread_basins():
        zero = jnp.zeros((tile_rows, basins), jnp.float32)
        carry = (zero,) * (scan_block + 1)
        for t, p in enumerate(near):
            if t > 0:
                idz_arrival(p).wait_recv()
            carry = sum_rows(p, carry)
        count, *totals = carry
        for b in range(scan_block):
            psend[b : b + 1, :] = jnp.sum(totals[b], axis=0, keepdims=True)
        pcount[...] = jnp.sum(count, axis=0, keepdims=True)

        def b_start(k, carry):
            b_copy(k).start()
            return carry

        lax.fori_loop(1, devices, b_start, 0, unroll=True)
        precv[me] = psend[:, owner_lanes(me)]

    for t in range(planes - 1):
        push_chunk(t)
        if t == 0:
            spread_basins()
            for late in range(early, planes):
                send_chunk(late)

    for p in range(planes):

        @pl.when(p != plane)
        def _():
            several(
                zrecv.at[p, pl.ds(0, hour_span(p))], z_send, z_recv.at[p]
            ).wait_recv()

    for h in range(hour_count):
        total = None
        for p in range(planes):
            if first_hour(p) <= h < first_hour(p) + hour_span(p):
                term = zrecv[p, h - first_hour(p)]
                total = term if total is None else total + term
        hourly_ref[h] = total

    in_arrival(plane).wait_recv()
    sums = chunk_sums(plane)
    for k in range(slots):

        @pl.when(k < span)
        def _():
            hourly_ref[base_hour + k] += sums[k]

    several(precv.at[pl.ds(0, devices - 1)], b_send, b_recv).wait_recv()
    hour_rows = lax.broadcasted_iota(jnp.int32, (hour_count, width), 0)
    total = jnp.zeros((hour_count, width), jnp.float32)
    for o in range(devices):
        for b in range(scan_block):
            hour = hours[o * scan_block + b]
            total = total + jnp.where(hour_rows == hour, precv[o, b : b + 1, :], 0.0)
    mean = total / pcount[:, owner_lanes(me)]
    mean = pltpu.roll(mean, (width - (me * owned) % width) % width, 1)
    basin_ref[...] = mean[:, :owned]

    several(plane_ids.at[pl.ds(0, members - 1)], id_send, id_recv).wait_send()
    several(all_ids.at[pl.ds(0, planes - 1)], idz_send, idz_recv.at[0]).wait_send()
    several(precv.at[pl.ds(0, devices - 1)], b_send, b_recv).wait_send()
    several(gather.at[:, pl.ds(0, members - 1)], in_send, in_recv.at[0]).wait_send()
    for n in sorted({hour_span(p) for p in range(planes)}):

        @pl.when(span == n)
        def _():
            several(
                part.at[pl.ds(0, planes - 1), pl.ds(0, n)], z_send, z_recv.at[0]
            ).wait_send()


def write_out(hourly_ref, basin_ref, hourly_out, basin_out, sem):
    pairs = ((hourly_ref, hourly_out), (basin_ref, basin_out))
    copies = [pltpu.make_async_copy(s, d, sem.at[n]) for n, (s, d) in enumerate(pairs)]
    for copy in copies:
        copy.start()
    for copy in copies:
        copy.wait()


def body(reflectivity, scan_hour, basin_ids):
    row_devices = lax.axis_size("row")
    col_devices = lax.axis_size("col")
    scan_block, grid_height, grid_width = reflectivity.shape
    tile_rows = grid_height // row_devices
    tile_cols = grid_width // col_devices
    scan_count = scan_hour.shape[0]
    hour_count = (scan_count + 10) // HOUR_SCANS + 1
    devices = row_devices * col_devices
    owned = grid_height * grid_width // (SEG * BASIN_ROWS) // devices
    planes = row_devices // CORES
    members = CORES * col_devices
    plane_scans = members * scan_block
    slots = max(
        hour_count
        - (scan_count - plane_scans * (p + 1)) // HOUR_SCANS
        - (p * plane_scans) // HOUR_SCANS
        for p in range(planes)
    )
    width = max(LANES, owned)
    dims = (row_devices, col_devices, hour_count, slots, tile_rows, tile_cols, owned)
    dma = pltpu.SemaphoreType.DMA
    f32 = jnp.float32
    anywhere = pl.BlockSpec(memory_space=pltpu.HBM)
    inside = pl.BlockSpec(memory_space=pltpu.VMEM)
    hourly, basin = pl.pallas_call(
        functools.partial(kernel, dims),
        out_shape=(
            jax.ShapeDtypeStruct((hour_count, tile_rows, tile_cols), f32),
            jax.ShapeDtypeStruct((hour_count, owned), f32),
        ),
        in_specs=[anywhere] * 3,
        out_specs=(inside, inside),
        scratch_shapes=[
            pltpu.VMEM(reflectivity.shape, f32),
            pltpu.SMEM(scan_hour.shape, jnp.int32),
            pltpu.VMEM(basin_ids.shape[::-1], jnp.int32),
            pltpu.VMEM((planes, members, scan_block, tile_rows, tile_cols), f32),
            pltpu.VMEM((planes, slots, tile_rows, tile_cols), f32),
            pltpu.VMEM((planes, slots, tile_rows, tile_cols), f32),
            pltpu.VMEM((members,) + basin_ids.shape[::-1], jnp.int32),
            pltpu.VMEM((planes, members) + basin_ids.shape[::-1], jnp.int32),
            pltpu.VMEM((scan_block, devices * owned), f32),
            pltpu.VMEM((1, devices * owned), f32),
            pltpu.VMEM((devices, scan_block, width), f32),
            pltpu.SemaphoreType.REGULAR((2,)),
            dma((3,)),
            dma((planes,)),
            dma,
            dma,
            dma((planes,)),
            dma,
            dma((planes,)),
            dma,
            dma,
            dma,
            dma((planes,)),
            dma,
            dma,
        ],
        compiler_params=pltpu.CompilerParams(
            collective_id=0, has_side_effects=True, vmem_limit_bytes=40 * 2**20
        ),
    )(*(pltpu.with_memory_space_constraint(v, pltpu.HBM) for v in (reflectivity, scan_hour, basin_ids.T)))
    hourly, basin = pl.pallas_call(
        write_out,
        out_shape=(
            jax.ShapeDtypeStruct(hourly.shape, f32),
            jax.ShapeDtypeStruct(basin.shape, f32),
        ),
        in_specs=[inside] * 2,
        out_specs=(anywhere, anywhere),
        scratch_shapes=[dma((2,))],
        compiler_params=pltpu.CompilerParams(vmem_limit_bytes=8 * 2**20),
    )(hourly, basin)
    return hourly, basin.T


def solution(mesh):
    placed = (P(("row", "col"), None, None), P(), P("row", "col"))
    return jax.shard_map(
        body,
        mesh=mesh,
        in_specs=placed,
        out_specs=(P(None, "row", "col"), P(("row", "col"), None)),
        check_vma=False,
    )
```

time: 23 us -> 21.2 us (0.922)
  Pallas kernels: 22.2 us -> 20.4 us
    pallas_call x1, Pallas kernels: 21.5 us -> 19.7 us  [body(): pl.pallas_call(functools.partial(kernel, dims), out_shape=(jax.ShapeDtype...]
where the time goes in v1:
time: 21.2 us; the launch traced here: 21 us
  Pallas kernels  20.4 us (96%)
  between operations  0.64 us (3%)
    pallas_call x1, Pallas kernels, body(): pl.pallas_call(functools.partial(kernel, dims), out_shape=(jax.ShapeDtype...  19.7 us
    pallas_call x1, Pallas kernels, body(): pl.pallas_call(write_out, out_shape=(jax.ShapeDtypeStruct(hourly.shape, f...  0.68 us

profile of v1, /device:TPU:0, one launch (start us, length us, event | category | flops | bytes accessed | tf_op | source)
XLA Modules:
  0.0 21.0 jit_solution(12726134112387275016)
XLA Ops:
  0.6 19.7 %shard_map.50 = (f32[4,32,256]{2,1,0:T(8,128)S(1)}, f32[4,8]{1,0:T(4,128)S(1)}) custom-call(f32[1,256,1024]{2,1,0:T(8,128)} %refl_ref.1, s32[32]{0:T(128)} %hour_ref.1, s32[2,32]{1,0:T(2,128)} %bitcast.2), custom_call_target="tpu_custom_call" | custom-call | tf_op jit(solution)/shard_map/pallas_call | solution.py:452
  20.3 0.7 %shard_map.51 = (f32[4,32,256]{2,1,0:T(8,128)}, f32[4,8]{1,0:T(4,128)}) custom-call(f32[4,32,256]{2,1,0:T(8,128)S(1)} %get-tuple-element.6.hourly_ref, f32[4,8]{1,0:T(4,128)S(1)} %get-tuple-element.7.basin_ref), custom_call_target="tpu_custom_call" | custom-call | tf_op jit(solution)/shard_map/pallas_call | solution.py:491

commit v2 on v1

--- a/solution.py
+++ b/solution.py
@@ -13,7 +13,6 @@
 HOUR_SCANS = 12
 CORES = 2
 LANES = 128
-HELD = 1
 MESH = pl.DeviceIdType.MESH
 
 slope_db = math.log(10.0) / 16.0
@@ -35,9 +34,11 @@
     zrecv,
     plane_ids,
     all_ids,
-    psend,
-    pcount,
-    precv,
+    seg_own,
+    seg_in,
+    seg_part,
+    zseg,
+    seg_hour,
     wave_sem,
     local_sem,
     load_sem,
@@ -50,8 +51,12 @@
     id_recv,
     idz_send,
     idz_recv,
-    b_send,
-    b_recv,
+    seg_send,
+    seg_recv,
+    zseg_send,
+    zseg_recv,
+    pair_send,
+    pair_recv,
 ):
     row_devices, col_devices, hour_count, slots, tile_rows, tile_cols, owned = dims
     planes = row_devices // CORES
@@ -61,8 +66,7 @@
     scan_count = hour_ref.shape[0]
     plane_scans = members * scan_block
     segs = tile_cols // SEG
-    basins = devices * owned
-    width = precv.shape[2]
+    all_segs, half_rows = seg_own.shape[2:]
 
     row = lax.axis_index("row")
     col = lax.axis_index("col")
@@ -91,13 +95,8 @@
             others.insert(0, 0)
         return others + [p]
 
-    def near_order(p):
-        return sorted(range(planes), key=lambda d: abs(d - p))
-
     orders = [chunk_order(p) for p in range(planes)]
     order = [by_plane([o[t] for o in orders]) for t in range(planes)]
-    nears = [near_order(p) for p in range(planes)]
-    near = [by_plane([o[t] for o in nears]) for t in range(planes)]
 
     def member_at(k):
         dc = k // col_devices
@@ -212,16 +211,53 @@
     def in_arrival(d):
         return several(gather.at[d, pl.ds(0, members - 1)], in_send, in_recv.at[d])
 
-    def send_chunk(t):
-        for k in range(1, members):
-            in_copy(order[t], k).start()
-
-    early = max(1, planes - HELD)
-    for t in range(early):
-        loads[t].wait()
+    def send_chunk(t, cores=range(CORES)):
+        for c in cores:
+            for k in range(max(1, c * col_devices), (c + 1) * col_devices):
+                in_copy(order[t], k).start()
+
+    def seg_copy(k):
+        other, r, q = member_at(k)
+        return pltpu.make_async_remote_copy(
+            src_ref=seg_own.at[other // col_devices],
+            dst_ref=seg_in.at[mine],
+            send_sem=seg_send,
+            recv_sem=seg_recv,
+            device_id=(r, q),
+            device_id_type=MESH,
+        )
+
+    def depth_of(raw):
+        return jnp.exp(raw * slope_db - offset_zr)
+
+    def sum_segments():
+        seg_row = lax.broadcasted_iota(jnp.int32, (all_segs, SEG), 0)
+        for b in range(scan_block):
+            for c in range(CORES):
+                rows = pl.ds(c * half_rows, half_rows)
+                total = jnp.zeros((all_segs, half_rows), jnp.float32)
+                for g in range(all_segs):
+                    depth = depth_of(frame[b, rows, g * SEG : (g + 1) * SEG])
+                    total = total + lax.dot_general(
+                        jnp.where(seg_row == g, 1.0, 0.0),
+                        depth,
+                        (((1,), (1,)), ((), ())),
+                        precision=lax.Precision.HIGHEST,
+                        preferred_element_type=jnp.float32,
+                    )
+                seg_own[c, b] = total
+
+    loads[0].wait()
+    send_chunk(0, [0])
+    for load in loads[1:]:
+        load.wait()
+    sum_segments()
+    for k in range(1, members):
+        seg_copy(k).start()
+    seg_in[mine] = seg_own[core]
+    send_chunk(0, range(1, CORES))
+    for t in range(1, planes):
         send_chunk(t)
-    for t in range(early, planes):
-        loads[t].wait()
 
 
     @pl.when(plane >= 2)
@@ -253,13 +289,10 @@
             src_ref=plane_ids,
             dst_ref=all_ids.at[plane],
             send_sem=idz_send,
-            recv_sem=idz_recv.at[plane],
+            recv_sem=idz_recv,
             device_id=(other * CORES + core, col),
             device_id_type=MESH,
         )
-
-    def idz_arrival(p):
-        return several(all_ids.at[p], idz_send, idz_recv.at[p])
 
     for k in range(1, planes):
         idz_copy(k).start()
@@ -280,44 +313,83 @@
             device_id_type=MESH,
         )
 
-    def owner_lanes(o):
-        return pl.ds(pl.multiple_of(((o * owned) // width) * width, width), width)
-
-    def b_copy(k):
-        other = (me + k) % devices
-        return pltpu.make_async_remote_copy(
-            src_ref=psend.at[:, owner_lanes(other)],
-            dst_ref=precv.at[me],
-            send_sem=b_send,
-            recv_sem=b_recv,
-            device_id=(other // col_devices, other % col_devices),
-            device_id_type=MESH,
-        )
-
-    def depth_of(raw):
-        return jnp.exp(raw * slope_db - offset_zr)
-
-    def sum_rows(p, carry):
-        lane = lax.broadcasted_iota(jnp.int32, (tile_rows, basins), 1)
-        count, *totals = carry
+    def zseg_copy(k):
+        other = (plane + k) % planes
+        return pltpu.make_async_remote_copy(
+            src_ref=seg_part,
+            dst_ref=zseg.at[plane],
+            send_sem=zseg_send,
+            recv_sem=zseg_recv,
+            device_id=(other * CORES + core, col),
+            device_id_type=MESH,
+        )
+
+    def pair_copy():
+        return pltpu.make_async_remote_copy(
+            src_ref=seg_hour.at[core],
+            dst_ref=seg_hour.at[core],
+            send_sem=pair_send,
+            recv_sem=pair_recv,
+            device_id=(plane * CORES + 1 - core, col),
+            device_id_type=MESH,
+        )
+
+    def reduce_segments():
+        several(seg_in.at[pl.ds(0, members - 1)], seg_send, seg_recv).wait_recv()
+        sums = [jnp.zeros((all_segs, half_rows), jnp.float32)] * slots
+        for i in range(members):
+            for b in range(scan_block):
+                hour = hours[plane * plane_scans + i * scan_block + b] - base_hour
+                for k in range(slots):
+                    sums[k] = sums[k] + jnp.where(hour == k, seg_in[i, b], 0.0)
+        for k in range(slots):
+            seg_part[k] = sums[k]
+            zseg[plane, k] = sums[k]
+        for k in range(1, planes):
+            zseg_copy(k).start()
+
+    def pair_segments():
+        several(zseg.at[pl.ds(0, planes - 1)], zseg_send, zseg_recv).wait_recv()
+        for h in range(hour_count):
+            total = None
+            for p in range(planes):
+                if first_hour(p) <= h < first_hour(p) + hour_span(p):
+                    term = zseg[p, h - first_hour(p)]
+                    total = term if total is None else total + term
+            seg_hour[core, h] = total
+        pair_copy().start()
+
+    def basin_means():
+        several(all_ids.at[pl.ds(0, planes - 1)], idz_send, idz_recv).wait_recv()
+        pair_copy().wait()
+        blocks = row_devices // CORES
+        halves = []
         for c in range(CORES):
-            depths = []
-            for b in range(scan_block):
-                rows = pl.ds(
-                    pl.multiple_of((p * CORES + c) * tile_rows, 8), tile_rows
-                )
-                depths.append(depth_of(frame[b, rows, :]))
-            tiles = [all_ids[p, c * col_devices + q] for q in range(col_devices)]
-            columns = jnp.transpose(jnp.concatenate(tiles, axis=0).astype(jnp.float32))
-            columns = columns.astype(jnp.int32)
-            for g in range(segs * col_devices):
-                hit = columns[:, g : g + 1] == lane
-                count = count + jnp.where(hit, float(SEG), 0.0)
-                for b in range(scan_block):
-                    part_depth = depths[b][:, g * SEG : (g + 1) * SEG]
-                    value = jnp.sum(part_depth, axis=1, keepdims=True)
-                    totals[b] = totals[b] + jnp.where(hit, value, 0.0)
-        return (count, *totals)
+            lanes = []
+            for r in range(c * blocks, (c + 1) * blocks):
+                first = (r % CORES) * col_devices
+                tiles = [all_ids[r // CORES, first + q] for q in range(col_devices)]
+                lanes.append(jnp.concatenate(tiles, axis=0))
+            halves.append(jnp.concatenate(lanes, axis=1))
+        place = lax.broadcasted_iota(jnp.int32, (owned, half_rows), 0)
+        zero = jnp.zeros((owned, half_rows), jnp.float32)
+        totals = [zero] * hour_count
+        count = zero
+        for n in range(owned):
+            hits = [half == me * owned + n for half in halves]
+            for h in range(hour_count):
+                kept = [jnp.where(hits[c], seg_hour[c, h], 0.0) for c in range(CORES)]
+                kept = jnp.sum(sum(kept), axis=0, keepdims=True)
+                totals[h] = jnp.where(place == n, kept, totals[h])
+            found = sum(jnp.where(hit, float(SEG), 0.0) for hit in hits)
+            count = jnp.where(place == n, jnp.sum(found, axis=0, keepdims=True), count)
+        pixels = jnp.sum(count, axis=1, keepdims=True)
+        lane = lax.broadcasted_iota(jnp.int32, (owned, LANES), 1)
+        means = jnp.zeros((owned, LANES), jnp.float32)
+        for h in range(hour_count):
+            mean = jnp.sum(totals[h], axis=1, keepdims=True) / pixels
+            means = jnp.where(lane == h, mean, means)
+        basin_ref[...] = jnp.transpose(means)[:hour_count, :]
 
     def chunk_sums(d):
         sums = [jnp.zeros((tile_rows, tile_cols), jnp.float32)] * slots
@@ -341,31 +413,12 @@
             def _():
                 z_copy(d, k).start()
 
-    def spread_basins():
-        zero = jnp.zeros((tile_rows, basins), jnp.float32)
-        carry = (zero,) * (scan_block + 1)
-        for t, p in enumerate(near):
-            if t > 0:
-                idz_arrival(p).wait_recv()
-            carry = sum_rows(p, carry)
-        count, *totals = carry
-        for b in range(scan_block):
-            psend[b : b + 1, :] = jnp.sum(totals[b], axis=0, keepdims=True)
-        pcount[...] = jnp.sum(count, axis=0, keepdims=True)
-
-        def b_start(k, carry):
-            b_copy(k).start()
-            return carry
-
-        lax.fori_loop(1, devices, b_start, 0, unroll=True)
-        precv[me] = psend[:, owner_lanes(me)]
-
+    reduce_segments()
     for t in range(planes - 1):
+        if t == planes - 2:
+            pair_segments()
         push_chunk(t)
-        if t == 0:
-            spread_basins()
-            for late in range(early, planes):
-                send_chunk(late)
+    basin_means()
 
     for p in range(planes):
 
@@ -391,20 +444,10 @@
         def _():
             hourly_ref[base_hour + k] += sums[k]
 
-    several(precv.at[pl.ds(0, devices - 1)], b_send, b_recv).wait_recv()
-    hour_rows = lax.broadcasted_iota(jnp.int32, (hour_count, width), 0)
-    total = jnp.zeros((hour_count, width), jnp.float32)
-    for o in range(devices):
-        for b in range(scan_block):
-            hour = hours[o * scan_block + b]
-            total = total + jnp.where(hour_rows == hour, precv[o, b : b + 1, :], 0.0)
-    mean = total / pcount[:, owner_lanes(me)]
-    mean = pltpu.roll(mean, (width - (me * owned) % width) % width, 1)
-    basin_ref[...] = mean[:, :owned]
-
     several(plane_ids.at[pl.ds(0, members - 1)], id_send, id_recv).wait_send()
-    several(all_ids.at[pl.ds(0, planes - 1)], idz_send, idz_recv.at[0]).wait_send()
-    several(precv.at[pl.ds(0, devices - 1)], b_send, b_recv).wait_send()
+    several(all_ids.at[pl.ds(0, planes - 1)], idz_send, idz_recv).wait_send()
+    several(seg_in.at[pl.ds(0, members - 1)], seg_send, seg_recv).wait_send()
+    several(zseg.at[pl.ds(0, planes - 1)], zseg_send, zseg_recv).wait_send()
     several(gather.at[:, pl.ds(0, members - 1)], in_send, in_recv.at[0]).wait_send()
     for n in sorted({hour_span(p) for p in range(planes)}):
 
@@ -443,7 +486,7 @@
         - (p * plane_scans) // HOUR_SCANS
         for p in range(planes)
     )
-    width = max(LANES, owned)
+    seg_shape = (grid_width // SEG, grid_height // CORES)
     dims = (row_devices, col_devices, hour_count, slots, tile_rows, tile_cols, owned)
     dma = pltpu.SemaphoreType.DMA
     f32 = jnp.float32
@@ -466,9 +509,11 @@
             pltpu.VMEM((planes, slots, tile_rows, tile_cols), f32),
             pltpu.VMEM((members,) + basin_ids.shape[::-1], jnp.int32),
             pltpu.VMEM((planes, members) + basin_ids.shape[::-1], jnp.int32),
-            pltpu.VMEM((scan_block, devices * owned), f32),
-            pltpu.VMEM((1, devices * owned), f32),
-            pltpu.VMEM((devices, scan_block, width), f32),
+            pltpu.VMEM((CORES, scan_block) + seg_shape, f32),
+            pltpu.VMEM((members, scan_block) + seg_shape, f32),
+            pltpu.VMEM((slots,) + seg_shape, f32),
+            pltpu.VMEM((planes, slots) + seg_shape, f32),
+            pltpu.VMEM((CORES, hour_count) + seg_shape, f32),
             pltpu.SemaphoreType.REGULAR((2,)),
             dma((3,)),
             dma((planes,)),
@@ -480,7 +525,11 @@
             dma,
             dma,
             dma,
-            dma((planes,)),
+            dma,
+            dma,
+            dma,
+            dma,
+            dma,
             dma,
             dma,
         ],

time: 21.2 us -> 20.7 us (0.976)
  Pallas kernels: 20.4 us -> 19.9 us
    pallas_call x1, Pallas kernels: 19.7 us -> 19.2 us  [body(): pl.pallas_call(functools.partial(kernel, dims), out_shape=(jax.ShapeDtype...]
where the time goes in v2:
time: 20.7 us; the launch traced here: 20.5 us
  Pallas kernels  19.9 us (96%)
  between operations  0.64 us (3%)
    pallas_call x1, Pallas kernels, body(): pl.pallas_call(functools.partial(kernel, dims), out_shape=(jax.ShapeDtype...  19.2 us
    pallas_call x1, Pallas kernels, body(): pl.pallas_call(write_out, out_shape=(jax.ShapeDtypeStruct(hourly.shape, f...  0.68 us

profile of v2, /device:TPU:0, one launch (start us, length us, event | category | flops | bytes accessed | tf_op | source)
XLA Modules:
  0.0 20.5 jit_solution(8623277181780957404)
XLA Ops:
  0.6 19.2 %shard_map.50 = (f32[4,32,256]{2,1,0:T(8,128)S(1)}, f32[4,8]{1,0:T(4,128)S(1)}) custom-call(f32[1,256,1024]{2,1,0:T(8,128)} %refl_ref.1, s32[32]{0:T(128)} %hour_ref.1, s32[2,32]{1,0:T(2,128)} %bitcast.2), custom_call_target="tpu_custom_call" | custom-call | tf_op jit(solution)/shard_map/pallas_call | solution.py:495
  19.9 0.7 %shard_map.51 = (f32[4,32,256]{2,1,0:T(8,128)}, f32[4,8]{1,0:T(4,128)}) custom-call(f32[4,32,256]{2,1,0:T(8,128)S(1)} %get-tuple-element.6.hourly_ref, f32[4,8]{1,0:T(4,128)S(1)} %get-tuple-element.7.basin_ref), custom_call_target="tpu_custom_call" | custom-call | tf_op jit(solution)/shard_map/pallas_call | solution.py:540

commit v3 on v2

--- a/solution.py
+++ b/solution.py
@@ -13,6 +13,7 @@
 HOUR_SCANS = 12
 CORES = 2
 LANES = 128
+PIECES = 2
 MESH = pl.DeviceIdType.MESH
 
 slope_db = math.log(10.0) / 16.0
@@ -65,7 +66,7 @@
     scan_block = gather.shape[2]
     scan_count = hour_ref.shape[0]
     plane_scans = members * scan_block
-    segs = tile_cols // SEG
+    piece_rows = tile_rows // PIECES
     all_segs, half_rows = seg_own.shape[2:]
 
     row = lax.axis_index("row")
@@ -197,24 +198,32 @@
             wave_sem.at[1], inc=1, device_id=along_z(-1), device_id_type=MESH
         )
 
-    def in_copy(d, k):
+    def piece(g):
+        return pl.ds(g * piece_rows, piece_rows)
+
+    def in_copy(d, g, k):
         other, r, q = member_at(k)
-        return pltpu.make_async_remote_copy(
-            src_ref=block_of(frame, d, other // col_devices, q),
-            dst_ref=gather.at[d, mine],
+        first = (d * CORES + other // col_devices) * tile_rows + g * piece_rows
+        rows = pl.ds(pl.multiple_of(first, 8), piece_rows)
+        cols = pl.ds(pl.multiple_of(q * tile_cols, 128), tile_cols)
+        return pltpu.make_async_remote_copy(
+            src_ref=frame.at[:, rows, cols],
+            dst_ref=gather.at[d, mine, :, piece(g)],
             send_sem=in_send,
-            recv_sem=in_recv.at[d],
+            recv_sem=in_recv.at[d, g],
             device_id=(r, q),
             device_id_type=MESH,
         )
 
-    def in_arrival(d):
-        return several(gather.at[d, pl.ds(0, members - 1)], in_send, in_recv.at[d])
-
-    def send_chunk(t, cores=range(CORES)):
-        for c in cores:
-            for k in range(max(1, c * col_devices), (c + 1) * col_devices):
-                in_copy(order[t], k).start()
+    def in_arrival(d, g):
+        ref = gather.at[d, pl.ds(0, members - 1), :, piece(g)]
+        return several(ref, in_send, in_recv.at[d, g])
+
+    far_first = sorted(range(1, members), key=lambda k: (-(k % col_devices), k))
+
+    def send_piece(t, g):
+        for k in far_first:
+            in_copy(order[t], g, k).start()
 
     def seg_copy(k):
         other, r, q = member_at(k)
@@ -231,33 +240,34 @@
         return jnp.exp(raw * slope_db - offset_zr)
 
     def sum_segments():
-        seg_row = lax.broadcasted_iota(jnp.int32, (all_segs, SEG), 0)
+        near_lane = lax.broadcasted_iota(jnp.int32, (SEG, LANES), 1)
         for b in range(scan_block):
             for c in range(CORES):
                 rows = pl.ds(c * half_rows, half_rows)
-                total = jnp.zeros((all_segs, half_rows), jnp.float32)
+                total = jnp.zeros((half_rows, LANES), jnp.float32)
                 for g in range(all_segs):
-                    depth = depth_of(frame[b, rows, g * SEG : (g + 1) * SEG])
-                    total = total + lax.dot_general(
-                        jnp.where(seg_row == g, 1.0, 0.0),
-                        depth,
-                        (((1,), (1,)), ((), ())),
-                        precision=lax.Precision.HIGHEST,
-                        preferred_element_type=jnp.float32,
-                    )
-                seg_own[c, b] = total
+                    rest = depth_of(frame[b, rows, g * SEG : (g + 1) * SEG])
+                    ones = jnp.where(near_lane == g, 1.0, 0.0).astype(jnp.bfloat16)
+                    for _ in range(3):
+                        head = rest.astype(jnp.bfloat16)
+                        rest = rest - head.astype(jnp.float32)
+                        total = total + jnp.dot(
+                            head, ones, preferred_element_type=jnp.float32
+                        )
+                seg_own[c, b] = jnp.transpose(total)[:all_segs]
 
     loads[0].wait()
-    send_chunk(0, [0])
+    send_piece(0, 0)
     for load in loads[1:]:
         load.wait()
     sum_segments()
     for k in range(1, members):
         seg_copy(k).start()
     seg_in[mine] = seg_own[core]
-    send_chunk(0, range(1, CORES))
-    for t in range(1, planes):
-        send_chunk(t)
+    for t in range(planes):
+        for g in range(PIECES):
+            if t or g:
+                send_piece(t, g)
 
 
     @pl.when(plane >= 2)
@@ -303,10 +313,10 @@
     base_hour = first_hour(plane)
     span = hour_span(plane)
 
-    def z_copy(d, k):
-        return pltpu.make_async_remote_copy(
-            src_ref=part.at[d, k],
-            dst_ref=zrecv.at[plane, k],
+    def z_copy(d, g, k):
+        return pltpu.make_async_remote_copy(
+            src_ref=part.at[d, k, piece(g)],
+            dst_ref=zrecv.at[plane, k, piece(g)],
             send_sem=z_send,
             recv_sem=z_recv.at[plane],
             device_id=(d * CORES + core, col),
@@ -391,33 +401,35 @@
             means = jnp.where(lane == h, mean, means)
         basin_ref[...] = jnp.transpose(means)[:hour_count, :]
 
-    def chunk_sums(d):
-        sums = [jnp.zeros((tile_rows, tile_cols), jnp.float32)] * slots
+    def piece_sums(d, g):
+        sums = [jnp.zeros((piece_rows, tile_cols), jnp.float32)] * slots
         for i in range(members):
             for b in range(scan_block):
                 hour = hours[plane * plane_scans + i * scan_block + b] - base_hour
-                depth = depth_of(gather[d, i, b])
+                depth = depth_of(gather[d, i, b, piece(g)])
                 for k in range(slots):
                     sums[k] = sums[k] + jnp.where(hour == k, depth, 0.0)
         return sums
 
-    def push_chunk(t):
+    def push_piece(t, g):
         d = order[t]
-        in_arrival(d).wait_recv()
-        sums = chunk_sums(d)
+        in_arrival(d, g).wait_recv()
+        sums = piece_sums(d, g)
         for k in range(slots):
-            part[d, k] = sums[k]
+            part[d, k, piece(g)] = sums[k]
         for k in range(slots):
 
             @pl.when(k < span)
             def _():
-                z_copy(d, k).start()
-
-    reduce_segments()
+                z_copy(d, g, k).start()
+
     for t in range(planes - 1):
-        if t == planes - 2:
-            pair_segments()
-        push_chunk(t)
+        for g in range(PIECES):
+            push_piece(t, g)
+            if t == 0 and g == 0:
+                reduce_segments()
+            if t == planes - 2 and g == 0:
+                pair_segments()
     basin_means()
 
     for p in range(planes):
@@ -436,19 +448,20 @@
                 total = term if total is None else total + term
         hourly_ref[h] = total
 
-    in_arrival(plane).wait_recv()
-    sums = chunk_sums(plane)
-    for k in range(slots):
-
-        @pl.when(k < span)
-        def _():
-            hourly_ref[base_hour + k] += sums[k]
+    for g in range(PIECES):
+        in_arrival(plane, g).wait_recv()
+        sums = piece_sums(plane, g)
+        for k in range(slots):
+
+            @pl.when(k < span)
+            def _():
+                hourly_ref[base_hour + k, piece(g)] += sums[k]
 
     several(plane_ids.at[pl.ds(0, members - 1)], id_send, id_recv).wait_send()
     several(all_ids.at[pl.ds(0, planes - 1)], idz_send, idz_recv).wait_send()
     several(seg_in.at[pl.ds(0, members - 1)], seg_send, seg_recv).wait_send()
     several(zseg.at[pl.ds(0, planes - 1)], zseg_send, zseg_recv).wait_send()
-    several(gather.at[:, pl.ds(0, members - 1)], in_send, in_recv.at[0]).wait_send()
+    several(gather.at[:, pl.ds(0, members - 1)], in_send, in_recv.at[0, 0]).wait_send()
     for n in sorted({hour_span(p) for p in range(planes)}):
 
         @pl.when(span == n)
@@ -519,7 +532,7 @@
             dma((planes,)),
             dma,
             dma,
-            dma((planes,)),
+            dma((planes, PIECES)),
             dma,
             dma((planes,)),
             dma,

time: 20.7 us -> 19.8 us (0.957)
  Pallas kernels: 19.9 us -> 19 us
    pallas_call x1, Pallas kernels: 19.2 us -> 18.3 us  [body(): pl.pallas_call(functools.partial(kernel, dims), out_shape=(jax.ShapeDtype...]
where the time goes in v3:
time: 19.8 us; the launch traced here: 19.7 us
  Pallas kernels  19 us (96%)
  between operations  0.64 us (3%)
    pallas_call x1, Pallas kernels, body(): pl.pallas_call(functools.partial(kernel, dims), out_shape=(jax.ShapeDtype...  18.3 us
    pallas_call x1, Pallas kernels, body(): pl.pallas_call(write_out, out_shape=(jax.ShapeDtypeStruct(hourly.shape, f...  0.68 us

profile of v3, /device:TPU:0, one launch (start us, length us, event | category | flops | bytes accessed | tf_op | source)
XLA Modules:
  0.0 19.7 jit_solution(4736139214161581171)
XLA Ops:
  0.6 18.3 %shard_map.50 = (f32[4,32,256]{2,1,0:T(8,128)S(1)}, f32[4,8]{1,0:T(4,128)S(1)}) custom-call(f32[1,256,1024]{2,1,0:T(8,128)} %refl_ref.1, s32[32]{0:T(128)} %hour_ref.1, s32[2,32]{1,0:T(2,128)} %bitcast.2), custom_call_target="tpu_custom_call" | custom-call | tf_op jit(solution)/shard_map/pallas_call | solution.py:508
  19.0 0.7 %shard_map.51 = (f32[4,32,256]{2,1,0:T(8,128)}, f32[4,8]{1,0:T(4,128)}) custom-call(f32[4,32,256]{2,1,0:T(8,128)S(1)} %get-tuple-element.6.hourly_ref, f32[4,8]{1,0:T(4,128)S(1)} %get-tuple-element.7.basin_ref), custom_call_target="tpu_custom_call" | custom-call | tf_op jit(solution)/shard_map/pallas_call | solution.py:553

commit v4 on v3

--- a/solution.py
+++ b/solution.py
@@ -125,11 +125,15 @@
         _, r, q = member_at(k)
         pl.semaphore_signal(barrier, inc=1, device_id=(r, q), device_id_type=MESH)
 
-    @pl.when(plane > 0)
+    greeter = core == CORES - 1
+    below = greeter & (plane > 0)
+    above = greeter & (plane < planes - 1)
+
+    @pl.when(below)
     def _():
         pl.semaphore_signal(barrier, inc=1, device_id=along_z(-1), device_id_type=MESH)
 
-    @pl.when(plane < planes - 1)
+    @pl.when(above)
     def _():
         pl.semaphore_signal(barrier, inc=1, device_id=along_z(1), device_id_type=MESH)
 
@@ -169,7 +173,7 @@
         zrecv[plane, k] = jnp.zeros((tile_rows, tile_cols), jnp.float32)
 
     load_ids.wait()
-    beside = jnp.where(plane > 0, 1, 0) + jnp.where(plane < planes - 1, 1, 0)
+    beside = jnp.where(below, 1, 0) + jnp.where(above, 1, 0)
     pl.semaphore_wait(barrier, members - 1 + beside)
 
     def id_copy(k):
@@ -186,13 +190,13 @@
     for k in range(1, members):
         id_copy(k).start()
 
-    @pl.when((plane == 1) & (plane < planes - 1))
+    @pl.when(greeter & (plane == 0))
     def _():
         pl.semaphore_signal(
             wave_sem.at[0], inc=1, device_id=along_z(1), device_id_type=MESH
         )
 
-    @pl.when((plane == planes - 2) & (plane > 0))
+    @pl.when(greeter & (plane == planes - 1))
     def _():
         pl.semaphore_signal(
             wave_sem.at[1], inc=1, device_id=along_z(-1), device_id_type=MESH
@@ -270,25 +274,39 @@
                 send_piece(t, g)
 
 
-    @pl.when(plane >= 2)
+    @pl.when(below)
     def _():
         pl.semaphore_wait(wave_sem.at[0], 1)
 
-        @pl.when(plane < planes - 1)
+        @pl.when(above)
         def _():
             pl.semaphore_signal(
                 wave_sem.at[0], inc=1, device_id=along_z(1), device_id_type=MESH
             )
 
-    @pl.when(plane < planes - 2)
+    @pl.when(above)
     def _():
         pl.semaphore_wait(wave_sem.at[1], 1)
 
-        @pl.when(plane > 0)
+        @pl.when(below)
         def _():
             pl.semaphore_signal(
                 wave_sem.at[1], inc=1, device_id=along_z(-1), device_id_type=MESH
             )
+
+    @pl.when(greeter)
+    def _():
+        for c in range(CORES - 1):
+            pl.semaphore_signal(
+                wave_sem.at[2],
+                inc=1,
+                device_id=(plane * CORES + c, col),
+                device_id_type=MESH,
+            )
+
+    @pl.when(jnp.logical_not(greeter))
+    def _():
+        pl.semaphore_wait(wave_sem.at[2], 1)
 
     several(plane_ids.at[pl.ds(0, members - 1)], id_send, id_recv).wait_recv()
     load_own_ids.wait()
@@ -323,16 +341,25 @@
             device_id_type=MESH,
         )
 
-    def zseg_copy(k):
+    def zseg_copy(k, n):
         other = (plane + k) % planes
         return pltpu.make_async_remote_copy(
-            src_ref=seg_part,
-            dst_ref=zseg.at[plane],
+            src_ref=seg_part.at[pl.ds(0, n)],
+            dst_ref=zseg.at[pl.ds(plane * slots, n)],
             send_sem=zseg_send,
             recv_sem=zseg_recv,
             device_id=(other * CORES + core, col),
             device_id_type=MESH,
         )
+
+    spans = sorted({hour_span(p) for p in range(planes)})
+
+    def by_span(action):
+        for n in spans:
+
+            @pl.when(span == n)
+            def _():
+                action(n)
 
     def pair_copy():
         return pltpu.make_async_remote_copy(
@@ -354,17 +381,27 @@
                     sums[k] = sums[k] + jnp.where(hour == k, seg_in[i, b], 0.0)
         for k in range(slots):
             seg_part[k] = sums[k]
-            zseg[plane, k] = sums[k]
-        for k in range(1, planes):
-            zseg_copy(k).start()
+            zseg[plane * slots + k] = sums[k]
+
+        def send(n):
+            for k in range(1, planes):
+                zseg_copy(k, n).start()
+
+        by_span(send)
 
     def pair_segments():
-        several(zseg.at[pl.ds(0, planes - 1)], zseg_send, zseg_recv).wait_recv()
+        for p in range(planes):
+            n = sum(hour_span(o) for o in range(planes) if o != p)
+
+            @pl.when(plane == p)
+            def _():
+                several(zseg.at[pl.ds(0, n)], zseg_send, zseg_recv).wait_recv()
+
         for h in range(hour_count):
             total = None
             for p in range(planes):
                 if first_hour(p) <= h < first_hour(p) + hour_span(p):
-                    term = zseg[p, h - first_hour(p)]
+                    term = zseg[p * slots + h - first_hour(p)]
                     total = term if total is None else total + term
             seg_hour[core, h] = total
         pair_copy().start()
@@ -428,8 +465,7 @@
             push_piece(t, g)
             if t == 0 and g == 0:
                 reduce_segments()
-            if t == planes - 2 and g == 0:
-                pair_segments()
+    pair_segments()
     basin_means()
 
     for p in range(planes):
@@ -460,15 +496,17 @@
     several(plane_ids.at[pl.ds(0, members - 1)], id_send, id_recv).wait_send()
     several(all_ids.at[pl.ds(0, planes - 1)], idz_send, idz_recv).wait_send()
     several(seg_in.at[pl.ds(0, members - 1)], seg_send, seg_recv).wait_send()
-    several(zseg.at[pl.ds(0, planes - 1)], zseg_send, zseg_recv).wait_send()
     several(gather.at[:, pl.ds(0, members - 1)], in_send, in_recv.at[0, 0]).wait_send()
-    for n in sorted({hour_span(p) for p in range(planes)}):
-
-        @pl.when(span == n)
-        def _():
-            several(
-                part.at[pl.ds(0, planes - 1), pl.ds(0, n)], z_send, z_recv.at[0]
-            ).wait_send()
+
+    def sums_sent(n):
+        several(
+            zseg.at[pl.ds(0, (planes - 1) * n)], zseg_send, zseg_recv
+        ).wait_send()
+        several(
+            part.at[pl.ds(0, planes - 1), pl.ds(0, n)], z_send, z_recv.at[0]
+        ).wait_send()
+
+    by_span(sums_sent)
 
 
 def write_out(hourly_ref, basin_ref, hourly_out, basin_out, sem):
@@ -525,9 +563,9 @@
             pltpu.VMEM((CORES, scan_block) + seg_shape, f32),
             pltpu.VMEM((members, scan_block) + seg_shape, f32),
             pltpu.VMEM((slots,) + seg_shape, f32),
-            pltpu.VMEM((planes, slots) + seg_shape, f32),
+            pltpu.VMEM((planes * slots,) + seg_shape, f32),
             pltpu.VMEM((CORES, hour_count) + seg_shape, f32),
-            pltpu.SemaphoreType.REGULAR((2,)),
+            pltpu.SemaphoreType.REGULAR((3,)),
             dma((3,)),
             dma((planes,)),
             dma,

time: 19.8 us -> 19 us (0.960)
  Pallas kernels: 19 us -> 18.2 us
    pallas_call x1, Pallas kernels: 18.3 us -> 17.5 us  [body(): pl.pallas_call(functools.partial(kernel, dims), out_shape=(jax.ShapeDtype...]
where the time goes in v4:
time: 19 us; the launch traced here: 18.8 us
  Pallas kernels  18.2 us (96%)
  between operations  0.64 us (3%)
    pallas_call x1, Pallas kernels, body(): pl.pallas_call(functools.partial(kernel, dims), out_shape=(jax.ShapeDtype...  17.5 us
    pallas_call x1, Pallas kernels, body(): pl.pallas_call(write_out, out_shape=(jax.ShapeDtypeStruct(hourly.shape, f...  0.68 us

profile of v4, /device:TPU:0, one launch (start us, length us, event | category | flops | bytes accessed | tf_op | source)
XLA Modules:
  0.0 18.8 jit_solution(7424058909599309392)
XLA Ops:
  0.6 17.5 %shard_map.50 = (f32[4,32,256]{2,1,0:T(8,128)S(1)}, f32[4,8]{1,0:T(4,128)S(1)}) custom-call(f32[1,256,1024]{2,1,0:T(8,128)} %refl_ref.1, s32[32]{0:T(128)} %hour_ref.1, s32[2,32]{1,0:T(2,128)} %bitcast.2), custom_call_target="tpu_custom_call" | custom-call | tf_op jit(solution)/shard_map/pallas_call | solution.py:546
  18.2 0.7 %shard_map.51 = (f32[4,32,256]{2,1,0:T(8,128)}, f32[4,8]{1,0:T(4,128)}) custom-call(f32[4,32,256]{2,1,0:T(8,128)S(1)} %get-tuple-element.6.hourly_ref, f32[4,8]{1,0:T(4,128)S(1)} %get-tuple-element.7.basin_ref), custom_call_target="tpu_custom_call" | custom-call | tf_op jit(solution)/shard_map/pallas_call | solution.py:591

commit v5 on v4

v5 whole, which is shorter than its diff:
```python
import functools
import math

import jax
import jax.numpy as jnp
from jax import lax
from jax.experimental import pallas as pl
from jax.experimental.pallas import tpu as pltpu
from jax.sharding import PartitionSpec as P

SEG = 128
BASIN_ROWS = 8
HOUR_SCANS = 12
CORES = 2
LANES = 128
SWAP_ROWS = 8
SHARE_AT = (1, 2)
MESH = pl.DeviceIdType.MESH

slope_db = math.log(10.0) / 16.0
offset_zr = math.log(200.0) / 1.6 + math.log(12.0)


def kernel(
    dims,
    refl_ref,
    hour_ref,
    ids_ref,
    hourly_ref,
    basin_ref,
    frame,
    hours,
    ids,
    gather,
    part,
    zrecv,
    plane_ids,
    all_ids,
    seg_own,
    seg_in,
    seg_part,
    zseg,
    seg_hour,
    swap_in,
    gsum,
    grecv,
    gpart,
    zgrecv,
    wave_sem,
    local_sem,
    load_sem,
    own_sem,
    in_send,
    in_recv,
    z_send,
    z_recv,
    id_send,
    id_recv,
    idz_recv,
    seg_send,
    seg_recv,
    zseg_send,
    zseg_recv,
    pair_send,
    pair_recv,
    swap_send,
    swap_recv,
    g_send,
    g_recv,
    zg_send,
    zg_recv,
):
    row_devices, col_devices, hour_count, slots, tile_rows, tile_cols, owned = dims
    planes = row_devices // CORES
    pairs = planes // 2
    members = CORES * col_devices
    devices = row_devices * col_devices
    scan_block = gather.shape[2]
    scan_count = hour_ref.shape[0]
    plane_scans = members * scan_block
    direct = tile_rows - SWAP_ROWS
    pieces = ((0, 8), (8, direct - 8))
    all_segs, half_rows = seg_own.shape[2:]
    pair_slots = gsum.shape[1]

    row = lax.axis_index("row")
    col = lax.axis_index("col")
    plane = row // CORES
    core = row % CORES
    mine = core * col_devices + col
    me = row * col_devices + col
    pair = plane // 2
    parity = plane % 2
    twin = plane + 1 - 2 * parity

    def first_hour(p):
        return (p * plane_scans) // HOUR_SCANS

    def hour_span(p):
        rest = scan_count - plane_scans - p * plane_scans
        return hour_count - rest // HOUR_SCANS - first_hour(p)

    def pair_hours(j):
        return first_hour(2 * j + 1) + hour_span(2 * j + 1) - first_hour(2 * j)

    def by_plane(table):
        value = table[0]
        for p in range(1, planes):
            value = jnp.where(plane == p, table[p], value)
        return value

    def chunk_order(p):
        others = sorted((d for d in range(planes) if d != p), key=lambda d: -abs(d - p))
        if 0 in others:
            others.remove(0)
            others.insert(0, 0)
        return others + [p]

    orders = [chunk_order(p) for p in range(planes)]
    order = [by_plane([o[t] for o in orders]) for t in range(planes)]
    swaps = [(pair + 1 + n) % pairs for n in range(pairs)]

    def member_at(k):
        dc = k // col_devices
        dq = k % col_devices
        half = col_devices // 2
        qq = ((col // 2 + dq // 2) % half) * 2 + (col + dq) % 2
        other = ((core + dc) % CORES) * col_devices + qq
        return other, plane * CORES + other // col_devices, other % col_devices

    def several(ref, send_sem, recv_sem):
        return pltpu.make_async_remote_copy(
            src_ref=ref,
            dst_ref=ref,
            send_sem=send_sem,
            recv_sem=recv_sem,
            device_id=((row + 1) % row_devices, col),
            device_id_type=MESH,
        )

    def signal(sem, r, q):
        pl.semaphore_signal(sem, inc=1, device_id=(r, q), device_id_type=MESH)

    def row_at(p):
        return p * CORES + core

    barrier = pltpu.get_barrier_semaphore()
    for k in range(1, members):
        _, r, q = member_at(k)
        signal(barrier, r, q)

    greeter = core == CORES - 1
    below = greeter & (plane > 0)
    above = greeter & (plane < planes - 1)

    @pl.when(below)
    def _():
        signal(barrier, row_at(plane - 1), col)

    @pl.when(above)
    def _():
        signal(barrier, row_at(plane + 1), col)

    def tile_at(d, c):
        return pl.multiple_of((d * CORES + c) * tile_rows, 8)

    def lanes_of(q):
        return pl.ds(pl.multiple_of(q * tile_cols, 128), tile_cols)

    def plane_rows(d, count=1):
        rows = CORES * tile_rows
        return pl.ds(pl.multiple_of(d * rows, 8), rows * count)

    load_ids = pltpu.make_async_copy(ids_ref, ids, local_sem.at[0])
    load_ids.start()
    for t, d in enumerate(order):
        pltpu.make_async_copy(
            refl_ref.at[:, plane_rows(d), :],
            frame.at[:, plane_rows(d), :],
            load_sem.at[min(t, 1)],
        ).start()

    def frame_loaded(late):
        rows = frame.at[:, plane_rows(0, planes - 1 if late else 1), :]
        pltpu.make_async_copy(rows, rows, load_sem.at[late]).wait()

    load_hours = pltpu.make_async_copy(hour_ref, hours, local_sem.at[1])
    load_hours.start()
    for d in range(planes):
        rows = pl.ds(tile_at(d, core), direct)
        pltpu.make_async_copy(
            refl_ref.at[:, rows, lanes_of(col)], gather.at[d, mine], own_sem
        ).start()

    for k in range(slots):
        zrecv[plane * slots + k] = jnp.zeros((direct, tile_cols), jnp.float32)

    load_ids.wait()
    plane_ids[mine] = ids[...]
    beside = jnp.where(below, 1, 0) + jnp.where(above, 1, 0)
    pl.semaphore_wait(barrier, members - 1 + beside)

    def id_copy(k):
        other, r, q = member_at(k)
        return pltpu.make_async_remote_copy(
            src_ref=ids,
            dst_ref=plane_ids.at[mine],
            send_sem=id_send,
            recv_sem=id_recv,
            device_id=(r, q),
            device_id_type=MESH,
        )

    for k in range(1, members):
        id_copy(k).start()

    @pl.when(greeter)
    def _():
        signal(wave_sem.at[3], row_at(twin), col)

    @pl.when(greeter & (plane == 0))
    def _():
        signal(wave_sem.at[0], row_at(plane + 1), col)

    @pl.when(greeter & (plane == planes - 1))
    def _():
        signal(wave_sem.at[1], row_at(plane - 1), col)

    def piece(g):
        return pl.ds(*pieces[g])

    def in_copy(d, g, k):
        other, r, q = member_at(k)
        first, count = pieces[g]
        rows = pl.ds(pl.multiple_of(tile_at(d, other // col_devices) + first, 8), count)
        return pltpu.make_async_remote_copy(
            src_ref=frame.at[:, rows, lanes_of(q)],
            dst_ref=gather.at[d, mine, :, piece(g)],
            send_sem=in_send,
            recv_sem=in_recv.at[d, g],
            device_id=(r, q),
            device_id_type=MESH,
        )

    def in_arrival(d, g):
        ref = gather.at[d, pl.ds(0, members - 1), :, piece(g)]
        return several(ref, in_send, in_recv.at[d, g])

    far_first = sorted(range(1, members), key=lambda k: (-(k % col_devices), k))

    def send_piece(t, g):
        for k in far_first:
            in_copy(order[t], g, k).start()

    def seg_copy(k):
        other, r, q = member_at(k)
        return pltpu.make_async_remote_copy(
            src_ref=seg_own.at[other // col_devices],
            dst_ref=seg_in.at[mine],
            send_sem=seg_send,
            recv_sem=seg_recv,
            device_id=(r, q),
            device_id_type=MESH,
        )

    def depth_of(raw):
        return jnp.exp(raw * slope_db - offset_zr)

    def sum_segments():
        near_lane = lax.broadcasted_iota(jnp.int32, (SEG, LANES), 1)
        for b in range(scan_block):
            for c in range(CORES):
                rows = pl.ds(c * half_rows, half_rows)
                total = jnp.zeros((half_rows, LANES), jnp.float32)
                for g in range(all_segs):
                    rest = depth_of(frame[b, rows, g * SEG : (g + 1) * SEG])
                    ones = jnp.where(near_lane == g, 1.0, 0.0).astype(jnp.bfloat16)
                    for _ in range(3):
                        head = rest.astype(jnp.bfloat16)
                        rest = rest - head.astype(jnp.float32)
                        total = total + jnp.dot(
                            head, ones, preferred_element_type=jnp.float32
                        )
                seg_own[c, b] = jnp.transpose(total)[:all_segs]

    frame_loaded(0)
    send_piece(0, 0)
    frame_loaded(1)
    sum_segments()
    for k in range(1, members):
        seg_copy(k).start()
    seg_in[mine] = seg_own[core]
    send_piece(0, 1)
    for t in range(1, planes - 1):
        for g in range(len(pieces)):
            send_piece(t, g)
    send_piece(planes - 1, 0)

    def tell_core(sem):
        @pl.when(greeter)
        def _():
            for c in range(CORES - 1):
                signal(sem, plane * CORES + c, col)

        @pl.when(jnp.logical_not(greeter))
        def _():
            pl.semaphore_wait(sem, 1)


    @pl.when(greeter)
    def _():
        pl.semaphore_wait(wave_sem.at[3], 1)

    tell_core(wave_sem.at[4])

    def swap_rows(d, c):
        return pl.ds(pl.multiple_of(tile_at(d, c) + direct, 8), SWAP_ROWS)

    def swap_copy(j, d, c, p, slot):
        return pltpu.make_async_remote_copy(
            src_ref=frame.at[:, swap_rows(d, c), :],
            dst_ref=swap_in.at[j, slot],
            send_sem=swap_send,
            recv_sem=swap_recv.at[j],
            device_id=(p * CORES + c, col),
            device_id_type=MESH,
        )

    for j in swaps:
        for c in range(CORES):
            swap_copy(j, 2 * j + 1 - parity, c, twin, 1 + core).start()
    for j in swaps:
        swap_copy(j, 2 * j + parity, 1 - core, plane, 0).start()


    @pl.when(below)
    def _():
        pl.semaphore_wait(wave_sem.at[0], 1)

        @pl.when(above)
        def _():
            signal(wave_sem.at[0], row_at(plane + 1), col)

    @pl.when(above)
    def _():
        pl.semaphore_wait(wave_sem.at[1], 1)

        @pl.when(below)
        def _():
            signal(wave_sem.at[1], row_at(plane - 1), col)

    tell_core(wave_sem.at[2])

    several(plane_ids.at[pl.ds(0, members - 1)], id_send, id_recv).wait_recv()

    plane_block = pl.ds(plane * members, members)
    for k in range(1, planes):
        pltpu.make_async_remote_copy(
            src_ref=plane_ids,
            dst_ref=all_ids.at[plane_block],
            send_sem=id_send,
            recv_sem=idz_recv,
            device_id=(row_at((plane + k) % planes), col),
            device_id_type=MESH,
        ).start()
    all_ids[plane_block] = plane_ids[...]
    load_hours.wait()
    pltpu.make_async_copy(gather.at[:, 0], gather.at[:, 0], own_sem).wait()

    base_hour = first_hour(plane)
    span = hour_span(plane)
    pair_base = first_hour(2 * pair)
    spans = sorted({hour_span(p) for p in range(planes)})

    def by_span(action):
        for n in spans:

            @pl.when(span == n)
            def _():
                action(n)

    def z_copy(d, g, k):
        return pltpu.make_async_remote_copy(
            src_ref=part.at[d, k, piece(g)],
            dst_ref=zrecv.at[plane * slots + k, piece(g)],
            send_sem=z_send,
            recv_sem=z_recv,
            device_id=(row_at(d), col),
            device_id_type=MESH,
        )

    def zseg_copy(k, n):
        return pltpu.make_async_remote_copy(
            src_ref=seg_part.at[pl.ds(0, n)],
            dst_ref=zseg.at[pl.ds(plane * slots, n)],
            send_sem=zseg_send,
            recv_sem=zseg_recv,
            device_id=(row_at((plane + k) % planes), col),
            device_id_type=MESH,
        )

    def pair_copy():
        return pltpu.make_async_remote_copy(
            src_ref=seg_hour.at[core],
            dst_ref=seg_hour.at[core],
            send_sem=pair_send,
            recv_sem=pair_recv,
            device_id=(plane * CORES + 1 - core, col),
            device_id_type=MESH,
        )

    def wait_slots(ref, send_sem, recv_sem):
        for p in range(planes):
            n = sum(hour_span(o) for o in range(planes) if o != p)

            @pl.when(plane == p)
            def _():
                several(ref.at[pl.ds(0, n)], send_sem, recv_sem).wait_recv()

    def sum_planes(ref, h):
        total = None
        for p in range(planes):
            if first_hour(p) <= h < first_hour(p) + hour_span(p):
                term = ref[p * slots + h - first_hour(p)]
                total = term if total is None else total + term
        return total

    def add_by_hour(sums, raw, p, member, b, base):
        hour = hours[p * plane_scans + member * scan_block + b] - base
        return [
            total + jnp.where(hour == k, raw, 0.0) for k, total in enumerate(sums)
        ]

    def reduce_segments():
        several(seg_in.at[pl.ds(0, members - 1)], seg_send, seg_recv).wait_recv()
        sums = [jnp.zeros((all_segs, half_rows), jnp.float32)] * slots
        for i in range(members):
            for b in range(scan_block):
                sums = add_by_hour(sums, seg_in[i, b], plane, i, b, base_hour)
        for k in range(slots):
            seg_part[k] = sums[k]
            zseg[plane * slots + k] = sums[k]

        def send(n):
            for k in range(1, planes):
                zseg_copy(k, n).start()

        by_span(send)

    def pair_segments():
        wait_slots(zseg, zseg_send, zseg_recv)
        for h in range(hour_count):
            seg_hour[core, h] = sum_planes(zseg, h)
        pair_copy().start()

    def basin_means():
        several(
            all_ids.at[pl.ds(0, (planes - 1) * members)], id_send, idz_recv
        ).wait_recv()
        pair_copy().wait()
        blocks = row_devices // CORES
        halves = []
        for c in range(CORES):
            lanes = []
            for r in range(c * blocks, (c + 1) * blocks):
                first = r * col_devices
                tiles = [all_ids[first + q] for q in range(col_devices)]
                lanes.append(jnp.concatenate(tiles, axis=0))
            halves.append(jnp.concatenate(lanes, axis=1))
        place = lax.broadcasted_iota(jnp.int32, (owned, half_rows), 0)
        zero = jnp.zeros((owned, half_rows), jnp.float32)
        totals = [zero] * hour_count
        count = zero
        for n in range(owned):
            hits = [half == me * owned + n for half in halves]
            for h in range(hour_count):
                kept = [jnp.where(hits[c], seg_hour[c, h], 0.0) for c in range(CORES)]
                kept = jnp.sum(sum(kept), axis=0, keepdims=True)
                totals[h] = jnp.where(place == n, kept, totals[h])
            found = sum(jnp.where(hit, float(SEG), 0.0) for hit in hits)
            count = jnp.where(place == n, jnp.sum(found, axis=0, keepdims=True), count)
        pixels = jnp.sum(count, axis=1, keepdims=True)
        lane = lax.broadcasted_iota(jnp.int32, (owned, LANES), 1)
        means = jnp.zeros((owned, LANES), jnp.float32)
        for h in range(hour_count):
            mean = jnp.sum(totals[h], axis=1, keepdims=True) / pixels
            means = jnp.where(lane == h, mean, means)
        basin_ref[...] = jnp.transpose(means)[:hour_count, :]

    def piece_sums(d, g):
        sums = [jnp.zeros((pieces[g][1], tile_cols), jnp.float32)] * slots
        for i in range(members):
            for b in range(scan_block):
                depth = depth_of(gather[d, i, b, piece(g)])
                sums = add_by_hour(sums, depth, plane, i, b, base_hour)
        return sums

    def push_piece(t, g):
        d = order[t]
        in_arrival(d, g).wait_recv()
        sums = piece_sums(d, g)
        for k in range(slots):
            part[d, k, piece(g)] = sums[k]
        for k in range(slots):

            @pl.when(k < span)
            def _():
                z_copy(d, g, k).start()

    def share_swap(n):
        j = swaps[n]
        several(swap_in.at[j], swap_send, swap_recv.at[j]).wait_recv()
        sums = [jnp.zeros((SWAP_ROWS, frame.shape[2]), jnp.float32)] * pair_slots
        for b in range(scan_block):
            own = frame[b, swap_rows(2 * j + parity, core), :]
            sources = (
                (own, plane, core),
                (swap_in[j, 0, b], plane, 1 - core),
                (swap_in[j, 1, b], twin, 0),
                (swap_in[j, 2, b], twin, 1),
            )
            for raw, p, c in sources:
                member = c * col_devices + col
                sums = add_by_hour(sums, depth_of(raw), p, member, b, pair_base)
        for k in range(pair_slots):
            gsum[j, k] = sums[k]
        for k in range(col_devices - 1, 0, -1):
            _, r, q = member_at(k)
            pltpu.make_async_remote_copy(
                src_ref=gsum.at[j, :, :, lanes_of(q)],
                dst_ref=grecv.at[j, col],
                send_sem=g_send,
                recv_sem=g_recv.at[j],
                device_id=(r, q),
                device_id_type=MESH,
            ).start()

    def join_swap(n):
        j = swaps[n]
        several(
            grecv.at[j, pl.ds(0, col_devices - 1)], g_send, g_recv.at[j]
        ).wait_recv()
        totals = []
        for k in range(pair_slots):
            total = gsum[j, k, :, lanes_of(col)]
            for m in range(1, col_devices):
                _, _, q = member_at(m)
                total = total + grecv[j, q, k]
            totals.append(total)
        if n < pairs - 1:
            for k in range(pair_slots):
                gpart[j, k] = totals[k]
            pltpu.make_async_remote_copy(
                src_ref=gpart.at[j],
                dst_ref=zgrecv.at[pair],
                send_sem=zg_send,
                recv_sem=zg_recv,
                device_id=(row_at(2 * j + parity), col),
                device_id_type=MESH,
            ).start()
        else:
            for k in range(pair_slots):
                zgrecv[pair, k] = totals[k]

    pushes = [(t, g) for t in range(planes - 1) for g in range(len(pieces))]
    for n, (t, g) in enumerate(pushes):
        push_piece(t, g)
        if n == 0:
            reduce_segments()
        if n in SHARE_AT:
            share_swap(SHARE_AT.index(n))
        if n == SHARE_AT[-1]:
            for m in range(len(SHARE_AT), pairs):
                share_swap(m)
            send_piece(planes - 1, 1)
    for n in range(pairs - 1):
        join_swap(n)
    pair_segments()
    basin_means()
    join_swap(pairs - 1)

    wait_slots(zrecv, z_send, z_recv)
    several(zgrecv.at[pl.ds(0, pairs - 1)], zg_send, zg_recv).wait_recv()
    for h in range(hour_count):
        hourly_ref[h, :direct] = sum_planes(zrecv, h)
        total = None
        for j in range(pairs):
            if first_hour(2 * j) <= h < first_hour(2 * j) + pair_hours(j):
                term = zgrecv[j, h - first_hour(2 * j)]
                total = term if total is None else total + term
        hourly_ref[h, direct:] = total

    for g in range(len(pieces)):
        in_arrival(plane, g).wait_recv()
        sums = piece_sums(plane, g)
        for k in range(slots):

            @pl.when(k < span)
            def _():
                hourly_ref[base_hour + k, piece(g)] += sums[k]

    several(
        all_ids.at[pl.ds(0, planes * members - 1)], id_send, id_recv
    ).wait_send()
    several(seg_in.at[pl.ds(0, members - 1)], seg_send, seg_recv).wait_send()
    several(
        gather.at[:, pl.ds(0, members - 1)], in_send, in_recv.at[0, 0]
    ).wait_send()
    several(swap_in, swap_send, swap_recv.at[0]).wait_send()
    several(
        grecv.at[:, pl.ds(0, col_devices - 1)], g_send, g_recv.at[0]
    ).wait_send()
    several(gpart.at[pl.ds(0, pairs - 1)], zg_send, zg_recv).wait_send()

    def sums_sent(n):
        several(
            zseg.at[pl.ds(0, (planes - 1) * n)], zseg_send, zseg_recv
        ).wait_send()
        several(
            part.at[pl.ds(0, planes - 1), pl.ds(0, n)], z_send, z_recv
        ).wait_send()

    by_span(sums_sent)


def write_out(hourly_ref, basin_ref, hourly_out, basin_out, sem):
    pairs = ((hourly_ref, hourly_out), (basin_ref, basin_out))
    copies = [pltpu.make_async_copy(s, d, sem.at[n]) for n, (s, d) in enumerate(pairs)]
    for copy in copies:
        copy.start()
    for copy in copies:
        copy.wait()


def body(reflectivity, scan_hour, basin_ids):
    row_devices = lax.axis_size("row")
    col_devices = lax.axis_size("col")
    scan_block, grid_height, grid_width = reflectivity.shape
    tile_rows = grid_height // row_devices
    tile_cols = grid_width // col_devices
    scan_count = scan_hour.shape[0]
    hour_count = (scan_count + 10) // HOUR_SCANS + 1
    devices = row_devices * col_devices
    owned = grid_height * grid_width // (SEG * BASIN_ROWS) // devices
    planes = row_devices // CORES
    pairs = planes // 2
    members = CORES * col_devices
    plane_scans = members * scan_block

    def span_of(first, last):
        rest = scan_count - plane_scans * (last + 1)
        return hour_count - rest // HOUR_SCANS - (first * plane_scans) // HOUR_SCANS

    slots = max(span_of(p, p) for p in range(planes))
    pair_slots = max(span_of(2 * j, 2 * j + 1) for j in range(pairs))
    seg_shape = (grid_width // SEG, grid_height // CORES)
    dims = (row_devices, col_devices, hour_count, slots, tile_rows, tile_cols, owned)
    direct = tile_rows - SWAP_ROWS
    dma = pltpu.SemaphoreType.DMA
    f32 = jnp.float32
    id_shape = basin_ids.shape[::-1]
    anywhere = pl.BlockSpec(memory_space=pltpu.HBM)
    inside = pl.BlockSpec(memory_space=pltpu.VMEM)
    hourly, basin = pl.pallas_call(
        functools.partial(kernel, dims),
        out_shape=(
            jax.ShapeDtypeStruct((hour_count, tile_rows, tile_cols), f32),
            jax.ShapeDtypeStruct((hour_count, owned), f32),
        ),
        in_specs=[anywhere] * 3,
        out_specs=(inside, inside),
        scratch_shapes=[
            pltpu.VMEM(reflectivity.shape, f32),
            pltpu.SMEM(scan_hour.shape, jnp.int32),
            pltpu.VMEM(id_shape, jnp.int32),
            pltpu.VMEM((planes, members, scan_block, direct, tile_cols), f32),
            pltpu.VMEM((planes, slots, direct, tile_cols), f32),
            pltpu.VMEM((planes * slots, direct, tile_cols), f32),
            pltpu.VMEM((members,) + id_shape, jnp.int32),
            pltpu.VMEM((planes * members,) + id_shape, jnp.int32),
            pltpu.VMEM((CORES, scan_block) + seg_shape, f32),
            pltpu.VMEM((members, scan_block) + seg_shape, f32),
            pltpu.VMEM((slots,) + seg_shape, f32),
            pltpu.VMEM((planes * slots,) + seg_shape, f32),
            pltpu.VMEM((CORES, hour_count) + seg_shape, f32),
            pltpu.VMEM((pairs, CORES + 1, scan_block, SWAP_ROWS, grid_width), f32),
            pltpu.VMEM((pairs, pair_slots, SWAP_ROWS, grid_width), f32),
            pltpu.VMEM((pairs, col_devices, pair_slots, SWAP_ROWS, tile_cols), f32),
            pltpu.VMEM((pairs, pair_slots, SWAP_ROWS, tile_cols), f32),
            pltpu.VMEM((pairs, pair_slots, SWAP_ROWS, tile_cols), f32),
            pltpu.SemaphoreType.REGULAR((5,)),
            dma((2,)),
            dma((2,)),
            dma,
            dma,
            dma((planes, 2)),
            dma,
            dma,
            dma,
            dma,
            dma,
            dma,
            dma,
            dma,
            dma,
            dma,
            dma,
            dma,
            dma((pairs,)),
            dma,
            dma((pairs,)),
            dma,
            dma,
        ],
        compiler_params=pltpu.CompilerParams(
            collective_id=0, has_side_effects=True, vmem_limit_bytes=40 * 2**20
        ),
    )(*(pltpu.with_memory_space_constraint(v, pltpu.HBM) for v in (reflectivity, scan_hour, basin_ids.T)))
    hourly, basin = pl.pallas_call(
        write_out,
        out_shape=(
            jax.ShapeDtypeStruct(hourly.shape, f32),
            jax.ShapeDtypeStruct(basin.shape, f32),
        ),
        in_specs=[inside] * 2,
        out_specs=(anywhere, anywhere),
        scratch_shapes=[dma((2,))],
        compiler_params=pltpu.CompilerParams(vmem_limit_bytes=8 * 2**20),
    )(hourly, basin)
    return hourly, basin.T


def solution(mesh):
    placed = (P(("row", "col"), None, None), P(), P("row", "col"))
    return jax.shard_map(
        body,
        mesh=mesh,
        in_specs=placed,
        out_specs=(P(None, "row", "col"), P(("row", "col"), None)),
        check_vma=False,
    )
```

time: 19 us -> 21.2 us (1.12)
  Pallas kernels: 18.2 us -> 20.4 us
    pallas_call x1, Pallas kernels: 17.5 us -> 19.7 us  [body(): pl.pallas_call(functools.partial(kernel, dims), out_shape=(jax.ShapeDtype...]
where the time goes in v5:
time: 21.2 us; the launch traced here: 21 us
  Pallas kernels  20.4 us (96%)
  between operations  0.64 us (3%)
    pallas_call x1, Pallas kernels, body(): pl.pallas_call(functools.partial(kernel, dims), out_shape=(jax.ShapeDtype...  19.7 us
    pallas_call x1, Pallas kernels, body(): pl.pallas_call(write_out, out_shape=(jax.ShapeDtypeStruct(hourly.shape, f...  0.68 us

profile of v5, /device:TPU:0, one launch (start us, length us, event | category | flops | bytes accessed | tf_op | source)
XLA Modules:
  0.0 21.0 jit_solution(16423279571650358124)
XLA Ops:
  0.6 19.7 %shard_map.50 = (f32[4,32,256]{2,1,0:T(8,128)S(1)}, f32[4,8]{1,0:T(4,128)S(1)}) custom-call(f32[1,256,1024]{2,1,0:T(8,128)} %refl_ref.1, s32[32]{0:T(128)} %hour_ref.1, s32[2,32]{1,0:T(2,128)} %bitcast.2), custom_call_target="tpu_custom_call" | custom-call | tf_op jit(solution)/shard_map/pallas_call | solution.py:664
  20.3 0.7 %shard_map.51 = (f32[4,32,256]{2,1,0:T(8,128)}, f32[4,8]{1,0:T(4,128)}) custom-call(f32[4,32,256]{2,1,0:T(8,128)S(1)} %get-tuple-element.6.hourly_ref, f32[4,8]{1,0:T(4,128)S(1)} %get-tuple-element.7.basin_ref), custom_call_target="tpu_custom_call" | custom-call | tf_op jit(solution)/shard_map/pallas_call | solution.py:719

commit v6 on v5

--- a/solution.py
+++ b/solution.py
@@ -13,8 +13,11 @@
 HOUR_SCANS = 12
 CORES = 2
 LANES = 128
-SWAP_ROWS = 8
-SHARE_AT = (1, 2)
+FIRST = (8, 16, 32)
+LATER = (16, 32)
+OWN = (16,)
+SWAP_ROWS = 16
+SHARE_AFTER = 1
 MESH = pl.DeviceIdType.MESH
 
 slope_db = math.log(10.0) / 16.0
@@ -44,12 +47,9 @@
     swap_in,
     gsum,
     grecv,
-    gpart,
-    zgrecv,
     wave_sem,
     local_sem,
     load_sem,
-    own_sem,
     in_send,
     in_recv,
     z_send,
@@ -67,20 +67,19 @@
     swap_recv,
     g_send,
     g_recv,
-    zg_send,
-    zg_recv,
 ):
     row_devices, col_devices, hour_count, slots, tile_rows, tile_cols, owned = dims
     planes = row_devices // CORES
-    pairs = planes // 2
     members = CORES * col_devices
     devices = row_devices * col_devices
     scan_block = gather.shape[2]
     scan_count = hour_ref.shape[0]
     plane_scans = members * scan_block
-    direct = tile_rows - SWAP_ROWS
-    pieces = ((0, 8), (8, direct - 8))
+    cuts = [FIRST] + [LATER] * (planes - 2) + [OWN]
+    pieces = [list(zip((0,) + ends[:-1], ends)) for ends in cuts]
+    piece_sem = [sum(map(len, cuts[:t])) for t in range(planes)]
     all_segs, half_rows = seg_own.shape[2:]
+    kept_rows = tile_rows - SWAP_ROWS
     pair_slots = gsum.shape[1]
 
     row = lax.axis_index("row")
@@ -90,8 +89,7 @@
     mine = core * col_devices + col
     me = row * col_devices + col
     pair = plane // 2
-    parity = plane % 2
-    twin = plane + 1 - 2 * parity
+    twin = plane + 1 - 2 * (plane % 2)
 
     def first_hour(p):
         return (p * plane_scans) // HOUR_SCANS
@@ -100,7 +98,7 @@
         rest = scan_count - plane_scans - p * plane_scans
         return hour_count - rest // HOUR_SCANS - first_hour(p)
 
-    def pair_hours(j):
+    def pair_span(j):
         return first_hour(2 * j + 1) + hour_span(2 * j + 1) - first_hour(2 * j)
 
     def by_plane(table):
@@ -118,7 +116,7 @@
 
     orders = [chunk_order(p) for p in range(planes)]
     order = [by_plane([o[t] for o in orders]) for t in range(planes)]
-    swaps = [(pair + 1 + n) % pairs for n in range(pairs)]
+    whole = [order[t] != twin for t in range(planes)]
 
     def member_at(k):
         dc = k // col_devices
@@ -145,7 +143,8 @@
         return p * CORES + core
 
     barrier = pltpu.get_barrier_semaphore()
-    for k in range(1, members):
+    far_first = sorted(range(1, members), key=lambda k: (-(k % col_devices), k))
+    for k in far_first:
         _, r, q = member_at(k)
         signal(barrier, r, q)
 
@@ -167,9 +166,9 @@
     def lanes_of(q):
         return pl.ds(pl.multiple_of(q * tile_cols, 128), tile_cols)
 
-    def plane_rows(d, count=1):
+    def plane_rows(d):
         rows = CORES * tile_rows
-        return pl.ds(pl.multiple_of(d * rows, 8), rows * count)
+        return pl.ds(pl.multiple_of(d * rows, 8), rows)
 
     load_ids = pltpu.make_async_copy(ids_ref, ids, local_sem.at[0])
     load_ids.start()
@@ -181,19 +180,17 @@
         ).start()
 
     def frame_loaded(late):
-        rows = frame.at[:, plane_rows(0, planes - 1 if late else 1), :]
+        count = (planes - 1 if late else 1) * CORES * tile_rows
+        rows = frame.at[:, pl.ds(0, count), :]
         pltpu.make_async_copy(rows, rows, load_sem.at[late]).wait()
 
     load_hours = pltpu.make_async_copy(hour_ref, hours, local_sem.at[1])
     load_hours.start()
-    for d in range(planes):
-        rows = pl.ds(tile_at(d, core), direct)
-        pltpu.make_async_copy(
-            refl_ref.at[:, rows, lanes_of(col)], gather.at[d, mine], own_sem
-        ).start()
-
     for k in range(slots):
-        zrecv[plane * slots + k] = jnp.zeros((direct, tile_cols), jnp.float32)
+        zrecv[plane * slots + k] = jnp.zeros((tile_rows, tile_cols), jnp.float32)
+        zrecv[twin * slots + k, kept_rows:] = jnp.zeros(
+            (SWAP_ROWS, tile_cols), jnp.float32
+        )
 
     load_ids.wait()
     plane_ids[mine] = ids[...]
@@ -226,31 +223,40 @@
     def _():
         signal(wave_sem.at[1], row_at(plane - 1), col)
 
-    def piece(g):
-        return pl.ds(*pieces[g])
-
-    def in_copy(d, g, k):
+    def piece(t, g):
+        first, end = pieces[t][g]
+        return pl.ds(first, end - first)
+
+    def in_copy(t, g, k):
         other, r, q = member_at(k)
-        first, count = pieces[g]
-        rows = pl.ds(pl.multiple_of(tile_at(d, other // col_devices) + first, 8), count)
+        d = order[t]
+        first, end = pieces[t][g]
+        top = pl.multiple_of(tile_at(d, other // col_devices) + first, 8)
         return pltpu.make_async_remote_copy(
-            src_ref=frame.at[:, rows, lanes_of(q)],
-            dst_ref=gather.at[d, mine, :, piece(g)],
+            src_ref=frame.at[:, pl.ds(top, end - first), lanes_of(q)],
+            dst_ref=gather.at[d, mine, :, piece(t, g)],
             send_sem=in_send,
-            recv_sem=in_recv.at[d, g],
+            recv_sem=in_recv.at[piece_sem[t] + g],
             device_id=(r, q),
             device_id_type=MESH,
         )
 
-    def in_arrival(d, g):
-        ref = gather.at[d, pl.ds(0, members - 1), :, piece(g)]
-        return several(ref, in_send, in_recv.at[d, g])
-
-    far_first = sorted(range(1, members), key=lambda k: (-(k % col_devices), k))
+    def in_arrival(t, g):
+        ref = gather.at[order[t], pl.ds(0, members - 1), :, piece(t, g)]
+        return several(ref, in_send, in_recv.at[piece_sem[t] + g])
+
+    def if_sent(t, g, action):
+        if pieces[t][g][0] < kept_rows:
+            action(t, g)
+        else:
+
+            @pl.when(whole[t])
+            def _():
+                action(t, g)
 
     def send_piece(t, g):
         for k in far_first:
-            in_copy(order[t], g, k).start()
+            in_copy(t, g, k).start()
 
     def seg_copy(k):
         other, r, q = member_at(k)
@@ -290,11 +296,14 @@
     for k in range(1, members):
         seg_copy(k).start()
     seg_in[mine] = seg_own[core]
-    send_piece(0, 1)
-    for t in range(1, planes - 1):
-        for g in range(len(pieces)):
-            send_piece(t, g)
-    send_piece(planes - 1, 0)
+    for t in range(planes):
+        for g in range(len(pieces[t])):
+            if t or g:
+                if_sent(t, g, send_piece)
+
+    for d in range(planes):
+        rows = pl.ds(tile_at(d, core), tile_rows)
+        gather[d, mine] = frame[:, rows, lanes_of(col)]
 
     def tell_core(sem):
         @pl.when(greeter)
@@ -314,23 +323,21 @@
     tell_core(wave_sem.at[4])
 
     def swap_rows(d, c):
-        return pl.ds(pl.multiple_of(tile_at(d, c) + direct, 8), SWAP_ROWS)
-
-    def swap_copy(j, d, c, p, slot):
+        return pl.ds(pl.multiple_of(tile_at(d, c) + kept_rows, 8), SWAP_ROWS)
+
+    def swap_copy(d, c, slot):
         return pltpu.make_async_remote_copy(
             src_ref=frame.at[:, swap_rows(d, c), :],
-            dst_ref=swap_in.at[j, slot],
+            dst_ref=swap_in.at[slot],
             send_sem=swap_send,
-            recv_sem=swap_recv.at[j],
-            device_id=(p * CORES + c, col),
-            device_id_type=MESH,
-        )
-
-    for j in swaps:
-        for c in range(CORES):
-            swap_copy(j, 2 * j + 1 - parity, c, twin, 1 + core).start()
-    for j in swaps:
-        swap_copy(j, 2 * j + parity, 1 - core, plane, 0).start()
+            recv_sem=swap_recv,
+            device_id=(d * CORES + c, col),
+            device_id_type=MESH,
+        )
+
+    for c in range(CORES):
+        swap_copy(twin, c, 1 + core).start()
+    swap_copy(plane, 1 - core, 0).start()
 
 
     @pl.when(below)
@@ -365,7 +372,6 @@
         ).start()
     all_ids[plane_block] = plane_ids[...]
     load_hours.wait()
-    pltpu.make_async_copy(gather.at[:, 0], gather.at[:, 0], own_sem).wait()
 
     base_hour = first_hour(plane)
     span = hour_span(plane)
@@ -379,13 +385,16 @@
             def _():
                 action(n)
 
-    def z_copy(d, g, k):
+    def side(p):
+        return jnp.where(p == twin, 1, 0)
+
+    def z_copy(t, g, k):
         return pltpu.make_async_remote_copy(
-            src_ref=part.at[d, k, piece(g)],
-            dst_ref=zrecv.at[plane * slots + k, piece(g)],
-            send_sem=z_send,
-            recv_sem=z_recv,
-            device_id=(row_at(d), col),
+            src_ref=part.at[order[t], k, piece(t, g)],
+            dst_ref=zrecv.at[plane * slots + k, piece(t, g)],
+            send_sem=z_send.at[side(order[t])],
+            recv_sem=z_recv.at[side(order[t])],
+            device_id=(row_at(order[t]), col),
             device_id_type=MESH,
         )
 
@@ -487,137 +496,126 @@
             means = jnp.where(lane == h, mean, means)
         basin_ref[...] = jnp.transpose(means)[:hour_count, :]
 
-    def piece_sums(d, g):
-        sums = [jnp.zeros((pieces[g][1], tile_cols), jnp.float32)] * slots
+    def piece_sums(t, g):
+        first, end = pieces[t][g]
+        sums = [jnp.zeros((end - first, tile_cols), jnp.float32)] * slots
         for i in range(members):
             for b in range(scan_block):
-                depth = depth_of(gather[d, i, b, piece(g)])
+                depth = depth_of(gather[order[t], i, b, piece(t, g)])
                 sums = add_by_hour(sums, depth, plane, i, b, base_hour)
         return sums
 
     def push_piece(t, g):
-        d = order[t]
-        in_arrival(d, g).wait_recv()
-        sums = piece_sums(d, g)
+        in_arrival(t, g).wait_recv()
+        sums = piece_sums(t, g)
         for k in range(slots):
-            part[d, k, piece(g)] = sums[k]
+            part[order[t], k, piece(t, g)] = sums[k]
         for k in range(slots):
 
             @pl.when(k < span)
             def _():
-                z_copy(d, g, k).start()
-
-    def share_swap(n):
-        j = swaps[n]
-        several(swap_in.at[j], swap_send, swap_recv.at[j]).wait_recv()
-        sums = [jnp.zeros((SWAP_ROWS, frame.shape[2]), jnp.float32)] * pair_slots
-        for b in range(scan_block):
-            own = frame[b, swap_rows(2 * j + parity, core), :]
-            sources = (
-                (own, plane, core),
-                (swap_in[j, 0, b], plane, 1 - core),
-                (swap_in[j, 1, b], twin, 0),
-                (swap_in[j, 2, b], twin, 1),
-            )
-            for raw, p, c in sources:
-                member = c * col_devices + col
-                sums = add_by_hour(sums, depth_of(raw), p, member, b, pair_base)
-        for k in range(pair_slots):
-            gsum[j, k] = sums[k]
-        for k in range(col_devices - 1, 0, -1):
+                z_copy(t, g, k).start()
+
+    def share_swap():
+        several(swap_in, swap_send, swap_recv).wait_recv()
+        for k in range(col_devices - 1, -1, -1):
             _, r, q = member_at(k)
-            pltpu.make_async_remote_copy(
-                src_ref=gsum.at[j, :, :, lanes_of(q)],
-                dst_ref=grecv.at[j, col],
-                send_sem=g_send,
-                recv_sem=g_recv.at[j],
-                device_id=(r, q),
-                device_id_type=MESH,
-            ).start()
-
-    def join_swap(n):
-        j = swaps[n]
-        several(
-            grecv.at[j, pl.ds(0, col_devices - 1)], g_send, g_recv.at[j]
-        ).wait_recv()
-        totals = []
-        for k in range(pair_slots):
-            total = gsum[j, k, :, lanes_of(col)]
-            for m in range(1, col_devices):
-                _, _, q = member_at(m)
-                total = total + grecv[j, q, k]
-            totals.append(total)
-        if n < pairs - 1:
-            for k in range(pair_slots):
-                gpart[j, k] = totals[k]
-            pltpu.make_async_remote_copy(
-                src_ref=gpart.at[j],
-                dst_ref=zgrecv.at[pair],
-                send_sem=zg_send,
-                recv_sem=zg_recv,
-                device_id=(row_at(2 * j + parity), col),
-                device_id_type=MESH,
-            ).start()
-        else:
-            for k in range(pair_slots):
-                zgrecv[pair, k] = totals[k]
-
-    pushes = [(t, g) for t in range(planes - 1) for g in range(len(pieces))]
-    for n, (t, g) in enumerate(pushes):
-        push_piece(t, g)
-        if n == 0:
-            reduce_segments()
-        if n in SHARE_AT:
-            share_swap(SHARE_AT.index(n))
-        if n == SHARE_AT[-1]:
-            for m in range(len(SHARE_AT), pairs):
-                share_swap(m)
-            send_piece(planes - 1, 1)
-    for n in range(pairs - 1):
-        join_swap(n)
+            lanes = lanes_of(q)
+            sums = [jnp.zeros((SWAP_ROWS, tile_cols), jnp.float32)] * pair_slots
+            for b in range(scan_block):
+                sources = (
+                    (frame[b, swap_rows(plane, core), lanes], plane, core),
+                    (swap_in[0, b, :, lanes], plane, 1 - core),
+                    (swap_in[1, b, :, lanes], twin, 0),
+                    (swap_in[2, b, :, lanes], twin, 1),
+                )
+                for raw, p, c in sources:
+                    member = c * col_devices + col
+                    sums = add_by_hour(sums, depth_of(raw), p, member, b, pair_base)
+            for n in range(pair_slots):
+                gsum[k, n] = sums[n]
+            if k > 0:
+                pltpu.make_async_remote_copy(
+                    src_ref=gsum.at[k],
+                    dst_ref=grecv.at[col],
+                    send_sem=g_send,
+                    recv_sem=g_recv,
+                    device_id=(r, q),
+                    device_id_type=MESH,
+                ).start()
+
+    def join_swap():
+        several(grecv.at[pl.ds(0, col_devices - 1)], g_send, g_recv).wait_recv()
+        for n in range(pair_slots):
+            total = gsum[0, n]
+            for k in range(1, col_devices):
+                _, _, q = member_at(k)
+                total = total + grecv[q, n]
+
+            @pl.when(n < pair_span(pair))
+            def _():
+                hourly_ref[pair_base + n, kept_rows:] += total
+
+    for t in range(planes - 1):
+        for g in range(len(pieces[t])):
+            if_sent(t, g, push_piece)
+            if t == 0 and g == 0:
+                reduce_segments()
+        if t == SHARE_AFTER:
+            share_swap()
     pair_segments()
     basin_means()
-    join_swap(pairs - 1)
-
-    wait_slots(zrecv, z_send, z_recv)
-    several(zgrecv.at[pl.ds(0, pairs - 1)], zg_send, zg_recv).wait_recv()
+
+    for p in range(planes):
+        other = p + 1 - 2 * (p % 2)
+        n = sum(hour_span(o) for o in range(planes) if o not in (p, other))
+
+        @pl.when(plane == p)
+        def _():
+            several(zrecv.at[pl.ds(0, n)], z_send.at[0], z_recv.at[0]).wait_recv()
+            several(
+                zrecv.at[pl.ds(0, hour_span(other)), pl.ds(0, kept_rows)],
+                z_send.at[1],
+                z_recv.at[1],
+            ).wait_recv()
+
     for h in range(hour_count):
-        hourly_ref[h, :direct] = sum_planes(zrecv, h)
-        total = None
-        for j in range(pairs):
-            if first_hour(2 * j) <= h < first_hour(2 * j) + pair_hours(j):
-                term = zgrecv[j, h - first_hour(2 * j)]
-                total = term if total is None else total + term
-        hourly_ref[h, direct:] = total
-
-    for g in range(len(pieces)):
-        in_arrival(plane, g).wait_recv()
-        sums = piece_sums(plane, g)
+        hourly_ref[h] = sum_planes(zrecv, h)
+
+    for g in range(len(pieces[-1])):
+        in_arrival(planes - 1, g).wait_recv()
+        sums = piece_sums(planes - 1, g)
         for k in range(slots):
 
             @pl.when(k < span)
             def _():
-                hourly_ref[base_hour + k, piece(g)] += sums[k]
+                hourly_ref[base_hour + k, piece(planes - 1, g)] += sums[k]
+
+    join_swap()
 
     several(
         all_ids.at[pl.ds(0, planes * members - 1)], id_send, id_recv
     ).wait_send()
     several(seg_in.at[pl.ds(0, members - 1)], seg_send, seg_recv).wait_send()
     several(
-        gather.at[:, pl.ds(0, members - 1)], in_send, in_recv.at[0, 0]
+        gather.at[pl.ds(0, planes - 1), pl.ds(0, members - 1)],
+        in_send,
+        in_recv.at[0],
     ).wait_send()
-    several(swap_in, swap_send, swap_recv.at[0]).wait_send()
-    several(
-        grecv.at[:, pl.ds(0, col_devices - 1)], g_send, g_recv.at[0]
-    ).wait_send()
-    several(gpart.at[pl.ds(0, pairs - 1)], zg_send, zg_recv).wait_send()
+    several(swap_in, swap_send, swap_recv).wait_send()
+    several(grecv.at[pl.ds(0, col_devices - 1)], g_send, g_recv).wait_send()
 
     def sums_sent(n):
         several(
             zseg.at[pl.ds(0, (planes - 1) * n)], zseg_send, zseg_recv
         ).wait_send()
         several(
-            part.at[pl.ds(0, planes - 1), pl.ds(0, n)], z_send, z_recv
+            part.at[pl.ds(0, planes - 2), pl.ds(0, n)], z_send.at[0], z_recv.at[0]
+        ).wait_send()
+        several(
+            part.at[0, pl.ds(0, n), pl.ds(0, kept_rows)],
+            z_send.at[1],
+            z_recv.at[1],
         ).wait_send()
 
     by_span(sums_sent)
@@ -643,7 +641,6 @@
     devices = row_devices * col_devices
     owned = grid_height * grid_width // (SEG * BASIN_ROWS) // devices
     planes = row_devices // CORES
-    pairs = planes // 2
     members = CORES * col_devices
     plane_scans = members * scan_block
 
@@ -652,10 +649,10 @@
         return hour_count - rest // HOUR_SCANS - (first * plane_scans) // HOUR_SCANS
 
     slots = max(span_of(p, p) for p in range(planes))
-    pair_slots = max(span_of(2 * j, 2 * j + 1) for j in range(pairs))
+    pair_slots = max(span_of(2 * j, 2 * j + 1) for j in range(planes // 2))
     seg_shape = (grid_width // SEG, grid_height // CORES)
     dims = (row_devices, col_devices, hour_count, slots, tile_rows, tile_cols, owned)
-    direct = tile_rows - SWAP_ROWS
+    piece_count = len(FIRST) + len(LATER) * (planes - 2) + len(OWN)
     dma = pltpu.SemaphoreType.DMA
     f32 = jnp.float32
     id_shape = basin_ids.shape[::-1]
@@ -673,9 +670,9 @@
             pltpu.VMEM(reflectivity.shape, f32),
             pltpu.SMEM(scan_hour.shape, jnp.int32),
             pltpu.VMEM(id_shape, jnp.int32),
-            pltpu.VMEM((planes, members, scan_block, direct, tile_cols), f32),
-            pltpu.VMEM((planes, slots, direct, tile_cols), f32),
-            pltpu.VMEM((planes * slots, direct, tile_cols), f32),
+            pltpu.VMEM((planes, members, scan_block, tile_rows, tile_cols), f32),
+            pltpu.VMEM((planes, slots, tile_rows, tile_cols), f32),
+            pltpu.VMEM((planes * slots, tile_rows, tile_cols), f32),
             pltpu.VMEM((members,) + id_shape, jnp.int32),
             pltpu.VMEM((planes * members,) + id_shape, jnp.int32),
             pltpu.VMEM((CORES, scan_block) + seg_shape, f32),
@@ -683,32 +680,27 @@
             pltpu.VMEM((slots,) + seg_shape, f32),
             pltpu.VMEM((planes * slots,) + seg_shape, f32),
             pltpu.VMEM((CORES, hour_count) + seg_shape, f32),
-            pltpu.VMEM((pairs, CORES + 1, scan_block, SWAP_ROWS, grid_width), f32),
-            pltpu.VMEM((pairs, pair_slots, SWAP_ROWS, grid_width), f32),
-            pltpu.VMEM((pairs, col_devices, pair_slots, SWAP_ROWS, tile_cols), f32),
-            pltpu.VMEM((pairs, pair_slots, SWAP_ROWS, tile_cols), f32),
-            pltpu.VMEM((pairs, pair_slots, SWAP_ROWS, tile_cols), f32),
+            pltpu.VMEM((CORES + 1, scan_block, SWAP_ROWS, grid_width), f32),
+            pltpu.VMEM((col_devices, pair_slots, SWAP_ROWS, tile_cols), f32),
+            pltpu.VMEM((col_devices, pair_slots, SWAP_ROWS, tile_cols), f32),
             pltpu.SemaphoreType.REGULAR((5,)),
             dma((2,)),
             dma((2,)),
             dma,
-            dma,
-            dma((planes, 2)),
-            dma,
-            dma,
-            dma,
-            dma,
-            dma,
-            dma,
-            dma,
-            dma,
-            dma,
-            dma,
-            dma,
-            dma,
-            dma((pairs,)),
-            dma,
-            dma((pairs,)),
+            dma((piece_count,)),
+            dma((2,)),
+            dma((2,)),
+            dma,
+            dma,
+            dma,
+            dma,
+            dma,
+            dma,
+            dma,
+            dma,
+            dma,
+            dma,
+            dma,
             dma,
             dma,
         ],

time: 21.2 us -> 18.9 us (0.89)
  Pallas kernels: 20.4 us -> 18.1 us
    pallas_call x1, Pallas kernels: 19.7 us -> 17.4 us  [body(): pl.pallas_call(functools.partial(kernel, dims), out_shape=(jax.ShapeDtype...]
where the time goes in v6:
time: 18.9 us; the launch traced here: 18.7 us
  Pallas kernels  18.1 us (96%)
  between operations  0.64 us (3%)
    pallas_call x1, Pallas kernels, body(): pl.pallas_call(functools.partial(kernel, dims), out_shape=(jax.ShapeDtype...  17.4 us
    pallas_call x1, Pallas kernels, body(): pl.pallas_call(write_out, out_shape=(jax.ShapeDtypeStruct(hourly.shape, f...  0.68 us

profile of v6, /device:TPU:0, one launch (start us, length us, event | category | flops | bytes accessed | tf_op | source)
XLA Modules:
  0.0 18.7 jit_solution(4708399541451048042)
XLA Ops:
  0.6 17.4 %shard_map.50 = (f32[4,32,256]{2,1,0:T(8,128)S(1)}, f32[4,8]{1,0:T(4,128)S(1)}) custom-call(f32[1,256,1024]{2,1,0:T(8,128)} %refl_ref.1, s32[32]{0:T(128)} %hour_ref.1, s32[2,32]{1,0:T(2,128)} %bitcast.2), custom_call_target="tpu_custom_call" | custom-call | tf_op jit(solution)/shard_map/pallas_call | solution.py:661
  18.0 0.7 %shard_map.51 = (f32[4,32,256]{2,1,0:T(8,128)}, f32[4,8]{1,0:T(4,128)}) custom-call(f32[4,32,256]{2,1,0:T(8,128)S(1)} %get-tuple-element.6.hourly_ref, f32[4,8]{1,0:T(4,128)S(1)} %get-tuple-element.7.basin_ref), custom_call_target="tpu_custom_call" | custom-call | tf_op jit(solution)/shard_map/pallas_call | solution.py:711

commit v7 on v6

--- a/solution.py
+++ b/solution.py
@@ -22,6 +22,21 @@
 
 slope_db = math.log(10.0) / 16.0
 offset_zr = math.log(200.0) / 1.6 + math.log(12.0)
+
+
+def sent_words(dims, scan_block, pair_slots, span):
+    row_devices, col_devices, hour_count, slots, tile_rows, tile_cols, owned = dims
+    planes = row_devices // CORES
+    members = CORES * col_devices
+    kept_rows = tile_rows - SWAP_ROWS
+    seg_words = row_devices * tile_rows // CORES * col_devices * tile_cols // SEG
+    chunk_rows = (planes - 2) * tile_rows + kept_rows
+    pixels = (members - 1) * (chunk_rows + kept_rows) * tile_cols * scan_block
+    segments = ((members - 1) * scan_block + hour_count) * seg_words
+    swapped = (CORES + 1) * SWAP_ROWS * col_devices * tile_cols * scan_block
+    shared = (col_devices - 1) * pair_slots * SWAP_ROWS * tile_cols
+    sums = span * (chunk_rows * tile_cols + (planes - 1) * seg_words)
+    return pixels + segments + swapped + shared + sums
 
 
 def kernel(
@@ -39,6 +54,7 @@
     zrecv,
     plane_ids,
     all_ids,
+    flat_ids,
     seg_own,
     seg_in,
     seg_part,
@@ -47,25 +63,20 @@
     swap_in,
     gsum,
     grecv,
+    spare,
     wave_sem,
     local_sem,
     load_sem,
-    in_send,
+    sent_sem,
     in_recv,
-    z_send,
     z_recv,
     id_send,
     id_recv,
     idz_recv,
-    seg_send,
     seg_recv,
-    zseg_send,
     zseg_recv,
-    pair_send,
     pair_recv,
-    swap_send,
     swap_recv,
-    g_send,
     g_recv,
 ):
     row_devices, col_devices, hour_count, slots, tile_rows, tile_cols, owned = dims
@@ -213,7 +224,7 @@
 
     @pl.when(greeter)
     def _():
-        signal(wave_sem.at[3], row_at(twin), col)
+        signal(wave_sem.at[2], row_at(twin), col)
 
     @pl.when(greeter & (plane == 0))
     def _():
@@ -235,7 +246,7 @@
         return pltpu.make_async_remote_copy(
             src_ref=frame.at[:, pl.ds(top, end - first), lanes_of(q)],
             dst_ref=gather.at[d, mine, :, piece(t, g)],
-            send_sem=in_send,
+            send_sem=sent_sem,
             recv_sem=in_recv.at[piece_sem[t] + g],
             device_id=(r, q),
             device_id_type=MESH,
@@ -243,7 +254,7 @@
 
     def in_arrival(t, g):
         ref = gather.at[order[t], pl.ds(0, members - 1), :, piece(t, g)]
-        return several(ref, in_send, in_recv.at[piece_sem[t] + g])
+        return several(ref, sent_sem, in_recv.at[piece_sem[t] + g])
 
     def if_sent(t, g, action):
         if pieces[t][g][0] < kept_rows:
@@ -263,7 +274,7 @@
         return pltpu.make_async_remote_copy(
             src_ref=seg_own.at[other // col_devices],
             dst_ref=seg_in.at[mine],
-            send_sem=seg_send,
+            send_sem=sent_sem,
             recv_sem=seg_recv,
             device_id=(r, q),
             device_id_type=MESH,
@@ -318,9 +329,9 @@
 
     @pl.when(greeter)
     def _():
-        pl.semaphore_wait(wave_sem.at[3], 1)
-
-    tell_core(wave_sem.at[4])
+        pl.semaphore_wait(wave_sem.at[2], 1)
+
+    tell_core(wave_sem.at[0])
 
     def swap_rows(d, c):
         return pl.ds(pl.multiple_of(tile_at(d, c) + kept_rows, 8), SWAP_ROWS)
@@ -329,7 +340,7 @@
         return pltpu.make_async_remote_copy(
             src_ref=frame.at[:, swap_rows(d, c), :],
             dst_ref=swap_in.at[slot],
-            send_sem=swap_send,
+            send_sem=sent_sem,
             recv_sem=swap_recv,
             device_id=(d * CORES + c, col),
             device_id_type=MESH,
@@ -356,7 +367,7 @@
         def _():
             signal(wave_sem.at[1], row_at(plane - 1), col)
 
-    tell_core(wave_sem.at[2])
+    tell_core(wave_sem.at[1])
 
     several(plane_ids.at[pl.ds(0, members - 1)], id_send, id_recv).wait_recv()
 
@@ -392,7 +403,7 @@
         return pltpu.make_async_remote_copy(
             src_ref=part.at[order[t], k, piece(t, g)],
             dst_ref=zrecv.at[plane * slots + k, piece(t, g)],
-            send_sem=z_send.at[side(order[t])],
+            send_sem=sent_sem,
             recv_sem=z_recv.at[side(order[t])],
             device_id=(row_at(order[t]), col),
             device_id_type=MESH,
@@ -402,7 +413,7 @@
         return pltpu.make_async_remote_copy(
             src_ref=seg_part.at[pl.ds(0, n)],
             dst_ref=zseg.at[pl.ds(plane * slots, n)],
-            send_sem=zseg_send,
+            send_sem=sent_sem,
             recv_sem=zseg_recv,
             device_id=(row_at((plane + k) % planes), col),
             device_id_type=MESH,
@@ -412,7 +423,7 @@
         return pltpu.make_async_remote_copy(
             src_ref=seg_hour.at[core],
             dst_ref=seg_hour.at[core],
-            send_sem=pair_send,
+            send_sem=sent_sem,
             recv_sem=pair_recv,
             device_id=(plane * CORES + 1 - core, col),
             device_id_type=MESH,
@@ -441,7 +452,7 @@
         ]
 
     def reduce_segments():
-        several(seg_in.at[pl.ds(0, members - 1)], seg_send, seg_recv).wait_recv()
+        several(seg_in.at[pl.ds(0, members - 1)], sent_sem, seg_recv).wait_recv()
         sums = [jnp.zeros((all_segs, half_rows), jnp.float32)] * slots
         for i in range(members):
             for b in range(scan_block):
@@ -457,25 +468,27 @@
         by_span(send)
 
     def pair_segments():
-        wait_slots(zseg, zseg_send, zseg_recv)
+        wait_slots(zseg, sent_sem, zseg_recv)
         for h in range(hour_count):
             seg_hour[core, h] = sum_planes(zseg, h)
         pair_copy().start()
 
-    def basin_means():
+    def lay_ids():
         several(
             all_ids.at[pl.ds(0, (planes - 1) * members)], id_send, idz_recv
         ).wait_recv()
-        pair_copy().wait()
         blocks = row_devices // CORES
-        halves = []
         for c in range(CORES):
             lanes = []
             for r in range(c * blocks, (c + 1) * blocks):
                 first = r * col_devices
                 tiles = [all_ids[first + q] for q in range(col_devices)]
                 lanes.append(jnp.concatenate(tiles, axis=0))
-            halves.append(jnp.concatenate(lanes, axis=1))
+            flat_ids[c] = jnp.concatenate(lanes, axis=1)
+
+    def basin_means():
+        pair_copy().wait_recv()
+        halves = [flat_ids[c] for c in range(CORES)]
         place = lax.broadcasted_iota(jnp.int32, (owned, half_rows), 0)
         zero = jnp.zeros((owned, half_rows), jnp.float32)
         totals = [zero] * hour_count
@@ -517,7 +530,7 @@
                 z_copy(t, g, k).start()
 
     def share_swap():
-        several(swap_in, swap_send, swap_recv).wait_recv()
+        several(swap_in, sent_sem, swap_recv).wait_recv()
         for k in range(col_devices - 1, -1, -1):
             _, r, q = member_at(k)
             lanes = lanes_of(q)
@@ -538,14 +551,14 @@
                 pltpu.make_async_remote_copy(
                     src_ref=gsum.at[k],
                     dst_ref=grecv.at[col],
-                    send_sem=g_send,
+                    send_sem=sent_sem,
                     recv_sem=g_recv,
                     device_id=(r, q),
                     device_id_type=MESH,
                 ).start()
 
     def join_swap():
-        several(grecv.at[pl.ds(0, col_devices - 1)], g_send, g_recv).wait_recv()
+        several(grecv.at[pl.ds(0, col_devices - 1)], sent_sem, g_recv).wait_recv()
         for n in range(pair_slots):
             total = gsum[0, n]
             for k in range(1, col_devices):
@@ -554,7 +567,7 @@
 
             @pl.when(n < pair_span(pair))
             def _():
-                hourly_ref[pair_base + n, kept_rows:] += total
+                hourly_ref[pair_base + n, kept_rows:] = total
 
     for t in range(planes - 1):
         for g in range(len(pieces[t])):
@@ -563,25 +576,9 @@
                 reduce_segments()
         if t == SHARE_AFTER:
             share_swap()
+    lay_ids()
     pair_segments()
-    basin_means()
-
-    for p in range(planes):
-        other = p + 1 - 2 * (p % 2)
-        n = sum(hour_span(o) for o in range(planes) if o not in (p, other))
-
-        @pl.when(plane == p)
-        def _():
-            several(zrecv.at[pl.ds(0, n)], z_send.at[0], z_recv.at[0]).wait_recv()
-            several(
-                zrecv.at[pl.ds(0, hour_span(other)), pl.ds(0, kept_rows)],
-                z_send.at[1],
-                z_recv.at[1],
-            ).wait_recv()
-
-    for h in range(hour_count):
-        hourly_ref[h] = sum_planes(zrecv, h)
-
+    hourly_ref[...] = jnp.zeros_like(hourly_ref)
     for g in range(len(pieces[-1])):
         in_arrival(planes - 1, g).wait_recv()
         sums = piece_sums(planes - 1, g)
@@ -589,36 +586,35 @@
 
             @pl.when(k < span)
             def _():
-                hourly_ref[base_hour + k, piece(planes - 1, g)] += sums[k]
+                hourly_ref[base_hour + k, piece(planes - 1, g)] = sums[k]
 
     join_swap()
+    basin_means()
+
+    for p in range(planes):
+        other = p + 1 - 2 * (p % 2)
+        n = sum(hour_span(o) for o in range(planes) if o not in (p, other))
+
+        @pl.when(plane == p)
+        def _():
+            several(zrecv.at[pl.ds(0, n)], sent_sem, z_recv.at[0]).wait_recv()
+            several(
+                zrecv.at[pl.ds(0, hour_span(other)), pl.ds(0, kept_rows)],
+                sent_sem,
+                z_recv.at[1],
+            ).wait_recv()
+
+    for h in range(hour_count):
+        hourly_ref[h] += sum_planes(zrecv, h)
 
     several(
         all_ids.at[pl.ds(0, planes * members - 1)], id_send, id_recv
     ).wait_send()
-    several(seg_in.at[pl.ds(0, members - 1)], seg_send, seg_recv).wait_send()
-    several(
-        gather.at[pl.ds(0, planes - 1), pl.ds(0, members - 1)],
-        in_send,
-        in_recv.at[0],
-    ).wait_send()
-    several(swap_in, swap_send, swap_recv).wait_send()
-    several(grecv.at[pl.ds(0, col_devices - 1)], g_send, g_recv).wait_send()
-
-    def sums_sent(n):
-        several(
-            zseg.at[pl.ds(0, (planes - 1) * n)], zseg_send, zseg_recv
-        ).wait_send()
-        several(
-            part.at[pl.ds(0, planes - 2), pl.ds(0, n)], z_send.at[0], z_recv.at[0]
-        ).wait_send()
-        several(
-            part.at[0, pl.ds(0, n), pl.ds(0, kept_rows)],
-            z_send.at[1],
-            z_recv.at[1],
-        ).wait_send()
-
-    by_span(sums_sent)
+    def all_sent(n):
+        count = sent_words(dims, scan_block, pair_slots, n) // (8 * LANES)
+        several(spare.at[pl.ds(0, count)], sent_sem, swap_recv).wait_send()
+
+    by_span(all_sent)
 
 
 def write_out(hourly_ref, basin_ref, hourly_out, basin_out, sem):
@@ -653,6 +649,7 @@
     seg_shape = (grid_width // SEG, grid_height // CORES)
     dims = (row_devices, col_devices, hour_count, slots, tile_rows, tile_cols, owned)
     piece_count = len(FIRST) + len(LATER) * (planes - 2) + len(OWN)
+    spare_count = sent_words(dims, scan_block, pair_slots, slots) // (8 * LANES)
     dma = pltpu.SemaphoreType.DMA
     f32 = jnp.float32
     id_shape = basin_ids.shape[::-1]
@@ -675,6 +672,7 @@
             pltpu.VMEM((planes * slots, tile_rows, tile_cols), f32),
             pltpu.VMEM((members,) + id_shape, jnp.int32),
             pltpu.VMEM((planes * members,) + id_shape, jnp.int32),
+            pltpu.VMEM((CORES,) + seg_shape, jnp.int32),
             pltpu.VMEM((CORES, scan_block) + seg_shape, f32),
             pltpu.VMEM((members, scan_block) + seg_shape, f32),
             pltpu.VMEM((slots,) + seg_shape, f32),
@@ -683,18 +681,13 @@
             pltpu.VMEM((CORES + 1, scan_block, SWAP_ROWS, grid_width), f32),
             pltpu.VMEM((col_devices, pair_slots, SWAP_ROWS, tile_cols), f32),
             pltpu.VMEM((col_devices, pair_slots, SWAP_ROWS, tile_cols), f32),
-            pltpu.SemaphoreType.REGULAR((5,)),
+            pltpu.VMEM((spare_count, 8, LANES), f32),
+            pltpu.SemaphoreType.REGULAR((3,)),
             dma((2,)),
             dma((2,)),
             dma,
             dma((piece_count,)),
             dma((2,)),
-            dma((2,)),
-            dma,
-            dma,
-            dma,
-            dma,
-            dma,
             dma,
             dma,
             dma,

time: 18.9 us -> 18.9 us (level)
  no operation moved by 1% of the time
where the time goes in v7:
time: 18.9 us; the launch traced here: 18.7 us
  Pallas kernels  18.1 us (96%)
  between operations  0.64 us (3%)
    pallas_call x1, Pallas kernels, body(): pl.pallas_call(functools.partial(kernel, dims), out_shape=(jax.ShapeDtype...  17.4 us
    pallas_call x1, Pallas kernels, body(): pl.pallas_call(write_out, out_shape=(jax.ShapeDtypeStruct(hourly.shape, f...  0.68 us

profile of v7, /device:TPU:0, one launch (start us, length us, event | category | flops | bytes accessed | tf_op | source)
XLA Modules:
  0.0 18.7 jit_solution(9296185114227838147)
XLA Ops:
  0.6 17.4 %shard_map.50 = (f32[4,32,256]{2,1,0:T(8,128)S(1)}, f32[4,8]{1,0:T(4,128)S(1)}) custom-call(f32[1,256,1024]{2,1,0:T(8,128)} %refl_ref.1, s32[32]{0:T(128)} %hour_ref.1, s32[2,32]{1,0:T(2,128)} %bitcast.2), custom_call_target="tpu_custom_call" | custom-call | tf_op jit(solution)/shard_map/pallas_call | solution.py:658
  18.0 0.7 %shard_map.51 = (f32[4,32,256]{2,1,0:T(8,128)}, f32[4,8]{1,0:T(4,128)}) custom-call(f32[4,32,256]{2,1,0:T(8,128)S(1)} %get-tuple-element.6.hourly_ref, f32[4,8]{1,0:T(4,128)S(1)} %get-tuple-element.7.basin_ref), custom_call_target="tpu_custom_call" | custom-call | tf_op jit(solution)/shard_map/pallas_call | solution.py:704

commit v8 on v7

--- a/solution.py
+++ b/solution.py
@@ -588,8 +588,8 @@
             def _():
                 hourly_ref[base_hour + k, piece(planes - 1, g)] = sums[k]
 
+    basin_means()
     join_swap()
-    basin_means()
 
     for p in range(planes):
         other = p + 1 - 2 * (p % 2)

time: 18.9 us -> 18.7 us (0.989)
  Pallas kernels: 18.1 us -> 17.9 us
    pallas_call x1, Pallas kernels: 17.4 us -> 17.2 us  [body(): pl.pallas_call(functools.partial(kernel, dims), out_shape=(jax.ShapeDtype...]
where the time goes in v8:
time: 18.7 us; the launch traced here: 18.5 us
  Pallas kernels  17.9 us (96%)
  between operations  0.64 us (3%)
    pallas_call x1, Pallas kernels, body(): pl.pallas_call(functools.partial(kernel, dims), out_shape=(jax.ShapeDtype...  17.2 us
    pallas_call x1, Pallas kernels, body(): pl.pallas_call(write_out, out_shape=(jax.ShapeDtypeStruct(hourly.shape, f...  0.68 us

profile of v8, /device:TPU:0, one launch (start us, length us, event | category | flops | bytes accessed | tf_op | source)
XLA Modules:
  0.0 18.5 jit_solution(7244554265163054883)
XLA Ops:
  0.6 17.2 %shard_map.50 = (f32[4,32,256]{2,1,0:T(8,128)S(1)}, f32[4,8]{1,0:T(4,128)S(1)}) custom-call(f32[1,256,1024]{2,1,0:T(8,128)} %refl_ref.1, s32[32]{0:T(128)} %hour_ref.1, s32[2,32]{1,0:T(2,128)} %bitcast.2), custom_call_target="tpu_custom_call" | custom-call | tf_op jit(solution)/shard_map/pallas_call | solution.py:658
  17.8 0.7 %shard_map.51 = (f32[4,32,256]{2,1,0:T(8,128)}, f32[4,8]{1,0:T(4,128)}) custom-call(f32[4,32,256]{2,1,0:T(8,128)S(1)} %get-tuple-element.6.hourly_ref, f32[4,8]{1,0:T(4,128)S(1)} %get-tuple-element.7.basin_ref), custom_call_target="tpu_custom_call" | custom-call | tf_op jit(solution)/shard_map/pallas_call | solution.py:704

commit v9 on v8

--- a/solution.py
+++ b/solution.py
@@ -266,7 +266,7 @@
                 action(t, g)
 
     def send_piece(t, g):
-        for k in far_first:
+        for k in sorted(range(1, members), key=lambda k: (-(k % col_devices), -k)):
             in_copy(t, g, k).start()
 
     def seg_copy(k):

time: 18.7 us -> 18.6 us (level)
  no operation moved by 1% of the time
where the time goes in v9:
time: 18.6 us; the launch traced here: 18.5 us
  Pallas kernels  17.9 us (96%)
  between operations  0.64 us (3%)
    pallas_call x1, Pallas kernels, body(): pl.pallas_call(functools.partial(kernel, dims), out_shape=(jax.ShapeDtype...  17.2 us
    pallas_call x1, Pallas kernels, body(): pl.pallas_call(write_out, out_shape=(jax.ShapeDtypeStruct(hourly.shape, f...  0.68 us

profile of v9, /device:TPU:0, one launch (start us, length us, event | category | flops | bytes accessed | tf_op | source)
XLA Modules:
  0.0 18.5 jit_solution(7449650761287194984)
XLA Ops:
  0.6 17.2 %shard_map.50 = (f32[4,32,256]{2,1,0:T(8,128)S(1)}, f32[4,8]{1,0:T(4,128)S(1)}) custom-call(f32[1,256,1024]{2,1,0:T(8,128)} %refl_ref.1, s32[32]{0:T(128)} %hour_ref.1, s32[2,32]{1,0:T(2,128)} %bitcast.2), custom_call_target="tpu_custom_call" | custom-call | tf_op jit(solution)/shard_map/pallas_call | solution.py:658
  17.8 0.7 %shard_map.51 = (f32[4,32,256]{2,1,0:T(8,128)}, f32[4,8]{1,0:T(4,128)}) custom-call(f32[4,32,256]{2,1,0:T(8,128)S(1)} %get-tuple-element.6.hourly_ref, f32[4,8]{1,0:T(4,128)S(1)} %get-tuple-element.7.basin_ref), custom_call_target="tpu_custom_call" | custom-call | tf_op jit(solution)/shard_map/pallas_call | solution.py:704

commit v10 on v9

--- a/solution.py
+++ b/solution.py
@@ -396,15 +396,12 @@
             def _():
                 action(n)
 
-    def side(p):
-        return jnp.where(p == twin, 1, 0)
-
     def z_copy(t, g, k):
         return pltpu.make_async_remote_copy(
             src_ref=part.at[order[t], k, piece(t, g)],
             dst_ref=zrecv.at[plane * slots + k, piece(t, g)],
             send_sem=sent_sem,
-            recv_sem=z_recv.at[side(order[t])],
+            recv_sem=z_recv,
             device_id=(row_at(order[t]), col),
             device_id_type=MESH,
         )
@@ -597,12 +594,9 @@
 
         @pl.when(plane == p)
         def _():
-            several(zrecv.at[pl.ds(0, n)], sent_sem, z_recv.at[0]).wait_recv()
-            several(
-                zrecv.at[pl.ds(0, hour_span(other)), pl.ds(0, kept_rows)],
-                sent_sem,
-                z_recv.at[1],
-            ).wait_recv()
+            rows = n * tile_rows + hour_span(other) * kept_rows
+            count = rows * tile_cols // (8 * LANES)
+            several(spare.at[pl.ds(0, count)], sent_sem, z_recv).wait_recv()
 
     for h in range(hour_count):
         hourly_ref[h] += sum_planes(zrecv, h)
@@ -687,7 +681,7 @@
             dma((2,)),
             dma,
             dma((piece_count,)),
-            dma((2,)),
+            dma,
             dma,
             dma,
             dma,

time: 18.6 us -> 18.6 us (level)
  no operation moved by 1% of the time
where the time goes in v10:
time: 18.6 us; the launch traced here: 18.5 us
  Pallas kernels  17.8 us (96%)
  between operations  0.64 us (3%)
    pallas_call x1, Pallas kernels, body(): pl.pallas_call(functools.partial(kernel, dims), out_shape=(jax.ShapeDtype...  17.2 us
    pallas_call x1, Pallas kernels, body(): pl.pallas_call(write_out, out_shape=(jax.ShapeDtypeStruct(hourly.shape, f...  0.68 us

profile of v10, /device:TPU:0, one launch (start us, length us, event | category | flops | bytes accessed | tf_op | source)
XLA Modules:
  0.0 18.5 jit_solution(4964832154606151489)
XLA Ops:
  0.6 17.2 %shard_map.50 = (f32[4,32,256]{2,1,0:T(8,128)S(1)}, f32[4,8]{1,0:T(4,128)S(1)}) custom-call(f32[1,256,1024]{2,1,0:T(8,128)} %refl_ref.1, s32[32]{0:T(128)} %hour_ref.1, s32[2,32]{1,0:T(2,128)} %bitcast.2), custom_call_target="tpu_custom_call" | custom-call | tf_op jit(solution)/shard_map/pallas_call | solution.py:652
  17.8 0.7 %shard_map.51 = (f32[4,32,256]{2,1,0:T(8,128)}, f32[4,8]{1,0:T(4,128)}) custom-call(f32[4,32,256]{2,1,0:T(8,128)S(1)} %get-tuple-element.6.hourly_ref, f32[4,8]{1,0:T(4,128)S(1)} %get-tuple-element.7.basin_ref), custom_call_target="tpu_custom_call" | custom-call | tf_op jit(solution)/shard_map/pallas_call | solution.py:698

commit v11 on v10

--- a/solution.py
+++ b/solution.py
@@ -119,7 +119,10 @@
         return value
 
     def chunk_order(p):
-        others = sorted((d for d in range(planes) if d != p), key=lambda d: -abs(d - p))
+        others = sorted(
+            (d for d in range(planes) if d != p),
+            key=lambda d: (d == p + 1 - 2 * (p % 2), abs(d - p)),
+        )
         if 0 in others:
             others.remove(0)
             others.insert(0, 0)

time: 18.6 us -> 18.6 us (level)
  no operation moved by 1% of the time
where the time goes in v11:
time: 18.6 us; the launch traced here: 18.5 us
  Pallas kernels  17.8 us (96%)
  between operations  0.64 us (3%)
    pallas_call x1, Pallas kernels, body(): pl.pallas_call(functools.partial(kernel, dims), out_shape=(jax.ShapeDtype...  17.2 us
    pallas_call x1, Pallas kernels, body(): pl.pallas_call(write_out, out_shape=(jax.ShapeDtypeStruct(hourly.shape, f...  0.68 us

profile of v11, /device:TPU:0, one launch (start us, length us, event | category | flops | bytes accessed | tf_op | source)
XLA Modules:
  0.0 18.5 jit_solution(270603829986486915)
XLA Ops:
  0.6 17.2 %shard_map.50 = (f32[4,32,256]{2,1,0:T(8,128)S(1)}, f32[4,8]{1,0:T(4,128)S(1)}) custom-call(f32[1,256,1024]{2,1,0:T(8,128)} %refl_ref.1, s32[32]{0:T(128)} %hour_ref.1, s32[2,32]{1,0:T(2,128)} %bitcast.2), custom_call_target="tpu_custom_call" | custom-call | tf_op jit(solution)/shard_map/pallas_call | solution.py:655
  17.8 0.7 %shard_map.51 = (f32[4,32,256]{2,1,0:T(8,128)}, f32[4,8]{1,0:T(4,128)}) custom-call(f32[4,32,256]{2,1,0:T(8,128)S(1)} %get-tuple-element.6.hourly_ref, f32[4,8]{1,0:T(4,128)S(1)} %get-tuple-element.7.basin_ref), custom_call_target="tpu_custom_call" | custom-call | tf_op jit(solution)/shard_map/pallas_call | solution.py:701
